TPU v7x, 128 devices: a whole 4x4x4 slice. The times are simulated.
128 devices in a mesh: dp: 32 (over z, y, x_lo), tensor: 4 (over x_hi, core).
Axes of the slice: x: 4 (x_hi: 2, x_lo: 2; x = x_hi * 2 + x_lo), y: 4, z: 4, core: 2. Of those that a mesh axis runs over, the one named last changes fastest.
Arguments:
- patches: bfloat16 [32768, 1280], P('dp'), may hold values from -27 to 27
- norm_gain: float32 [1280], replicated, may hold values from 0.1 to 1.9
- norm_bias: float32 [1280], replicated, may hold values from -3 to 3
- first_weight: bfloat16 [5120, 5120], P(None, 'tensor'), may hold values from -0.078125 to 0.078125
- first_bias: float32 [5120], P('tensor'), may hold values from -3 to 3
- second_weight: bfloat16 [5120, 8192], P('tensor', 'dp'), may hold values from -0.078125 to 0.078125
- second_bias: float32 [8192], P('tensor'), may hold values from -2 to 2
- text_embeds: bfloat16 [16384, 8192], P('dp', 'tensor'), may hold values from -36 to 36
- final_gain: float32 [8192], P('tensor'), may hold values from 0.1 to 1.9
- image_grids: int32 [32, 4, 2], replicated, may hold values from 2 to 8, as said below
- routing: int32 [32, 4], replicated, may hold values from 0 to 3, each once within a row
Outputs:
- embeddings: bfloat16 [16384, 8192], P('dp', 'tensor')
- normed: bfloat16 [16384, 8192], P('dp', 'tensor')
Inputs may be any that keep to these rules, and one draw needn't show every extreme that they name: `image_grids`: each image is a grid of 3 to 8 rows by 2 to 8 columns of merged tokens; in every draw some image is 8 by 8. `routing`: each row names every offset 0 to 3 once.
All inputs are finite; a program needn't handle non-finite values.
Results may differ from a plain program's by a relative error of at most 0.006.
Values may be sent and summed in bfloat16 or wider, within the bound.
No kernel may reach another device: no remote copies, remote signals or barrier semaphores. Data moves between devices by JAX's collectives and lax.ppermute only.
A program may use at most 128 MiB of HBM per device.

v0:
```python
import itertools

import jax
import jax.numpy as jnp
import numpy as np
from jax import lax
from jax.experimental import pallas as pl
from jax.experimental.pallas import tpu as pltpu
from jax.sharding import Mesh, PartitionSpec as P


D = 8192
EPS = 1e-06
AXES = ("z", "y", "xl", "xh", "c")
SIZES = {"z": 4, "y": 4, "xl": 2, "xh": 2, "c": 2}
SHARDS = 32
BLOCKS = 4
CAP = 64
ROWS = BLOCKS * CAP
BF = jnp.bfloat16
F32 = jnp.float32
VMEM = pl.BlockSpec(memory_space=pltpu.VMEM)
SMEM = pl.BlockSpec(memory_space=pltpu.SMEM)
ANY = pl.BlockSpec(memory_space=pl.ANY)


def shift(value, **deltas):
    axes = tuple(a for a in AXES if a in deltas)
    sizes = [SIZES[a] for a in axes]
    pairs = []
    for src in itertools.product(*[range(s) for s in sizes]):
        dst = [(i + deltas[a]) % s for i, a, s in zip(src, axes, sizes)]
        pairs.append((int(np.ravel_multi_index(src, sizes)), int(np.ravel_multi_index(dst, sizes))))
    return lax.ppermute(value, axes, pairs)


def shift_dp(value, distance):
    pairs = [(i, (i + distance) % SHARDS) for i in range(SHARDS)]
    return lax.ppermute(value, ("z", "y", "xl"), pairs)


def place(idx_ref):
    i = idx_ref[0]
    return i >> 5, (i >> 3) & 3, (i >> 2) & 1, (i >> 1) & 1, i & 1, i >> 2


def block_of(routing_ref, shard, offset):
    block = jnp.int32(0)
    for b in range(1, BLOCKS):
        block = jnp.where(routing_ref[shard, b] == offset, b, block)
    return block


def first_kernel(idx_ref, routing_ref, patches_ref, gain_ref, bias_ref, w_ref, b_ref, o0, o1, o2, o3, raw, scr, merged, sems):
    shard = place(idx_ref)[5]
    width = patches_ref.shape[1]
    cut = w_ref.shape[1]
    step = pl.program_id(0)

    def fetch(k):
        block = block_of(routing_ref, shard, k)
        rows = pl.ds(pl.multiple_of(block * ROWS, ROWS), ROWS)
        return pltpu.make_async_copy(patches_ref.at[rows, :], raw.at[k], sems.at[k])

    @pl.when(step == 0)
    def _():
        for k in range(BLOCKS):
            fetch(k).start()
        for k in range(BLOCKS):
            fetch(k).wait()
            x = raw[k].astype(F32)
            centered = x - jnp.mean(x, axis=-1, keepdims=True)
            variance = jnp.mean(centered * centered, axis=-1, keepdims=True)
            normed = centered * lax.rsqrt(variance + EPS) * gain_ref[...][None] + bias_ref[...][None]
            for t in range(width // 128):
                scr[t] = normed[:, t * 128 : (t + 1) * 128]
            for j in range(4):
                for t in range(width // 128):
                    at = j * width + t * 128
                    merged[k * CAP : (k + 1) * CAP, at : at + 128] = scr[t, pl.ds(j, CAP, stride=4), :].astype(BF)

    h = jnp.dot(merged[...], w_ref[...], preferred_element_type=F32)
    h = h + b_ref[pl.ds(pl.multiple_of(step * cut, cut), cut)][None]
    h = (0.5 * h * (1.0 + lax.erf(h * np.float32(np.sqrt(0.5))))).astype(BF)
    for k, o in enumerate((o0, o1, o2, o3)):
        o[...] = h[k * CAP : (k + 1) * CAP, :]


def first_product(idx, routing, patches, gain, bias, weight, bias1):
    depth, width = weight.shape
    cut = 256
    out = jax.ShapeDtypeStruct((CAP, width), BF)
    return pl.pallas_call(
        first_kernel,
        grid=(width // cut,),
        in_specs=[SMEM, SMEM, ANY, VMEM, VMEM, pl.BlockSpec((depth, cut), lambda n: (0, n)), VMEM],
        out_specs=[pl.BlockSpec((CAP, cut), lambda n: (0, n))] * BLOCKS,
        out_shape=[out] * BLOCKS,
        scratch_shapes=[
            pltpu.VMEM((BLOCKS, ROWS, patches.shape[1]), BF),
            pltpu.VMEM((patches.shape[1] // 128, ROWS, 128), F32),
            pltpu.VMEM((ROWS, depth), BF),
            pltpu.SemaphoreType.DMA((BLOCKS,)),
        ],
        compiler_params=pltpu.CompilerParams(vmem_limit_bytes=40 << 20),
        name="first_product",
    )(idx, routing, patches, gain, bias, weight, bias1)


CHUNKS = tuple((dz, dx) for dz in range(4) for dx in range(2))


def second_kernel(idx_ref, *refs):
    pieces = refs[:4]
    weights = refs[4:12]
    keep, send, rows = refs[12:]
    z, _, xl, xh, c, _ = place(idx_ref)
    for i in range(2):
        rows[i * ROWS : i * ROWS + CAP, :] = pieces[2 * i][...]
        rows[i * ROWS + CAP : (i + 1) * ROWS, :] = pieces[2 * i + 1][...]
    for (dz, dx), w in zip(CHUNKS, weights):
        group = (z - dz) & 3
        column = pl.multiple_of((xl ^ dx) * 256, 256)
        side = (group >> 1) ^ xh
        other = (group & 1) ^ c
        values = [
            jnp.dot(rows[i * ROWS : (i + 1) * ROWS, :], w[...], preferred_element_type=F32).astype(BF) for i in range(2)
        ]

        @pl.when(other == 0)
        def _():
            for i, v in enumerate(values):
                keep[side, i * ROWS : (i + 1) * ROWS, pl.ds(column, 256)] = v

        @pl.when(other == 1)
        def _():
            for i, v in enumerate(values):
                send[side, i * ROWS : (i + 1) * ROWS, pl.ds(column, 256)] = v


def second_product(idx, pieces, weights):
    out = jax.ShapeDtypeStruct((2, 2 * ROWS, 512), BF)
    return pl.pallas_call(
        second_kernel,
        in_specs=[SMEM] + [VMEM] * 12,
        out_specs=[VMEM, VMEM],
        out_shape=[out, out],
        scratch_shapes=[pltpu.VMEM((2 * ROWS, weights[0].shape[0]), BF)],
        compiler_params=pltpu.CompilerParams(vmem_limit_bytes=40 << 20),
    )(idx, *pieces, *weights)


def row_sums(v):
    ones = jnp.ones((8, v.shape[1]), F32)
    return lax.dot_general(ones, v * v, (((1,), (1,)), ((), ())), precision=lax.Precision.HIGHEST, preferred_element_type=F32)


def text_kernel(text_ref, out_ref, sum_ref):
    value = text_ref[...]
    out_ref[...] = value
    sum_ref[...] = row_sums(value.astype(F32))


def splice_kernel(idx_ref, routing_ref, grids_ref, *refs):
    stay = refs[:4]
    cross = refs[4:8]
    bias_ref, text_ref, _, out_ref, sum_ref = refs[8:]
    _, y, _, _, _, shard = place(idx_ref)
    row = lax.broadcasted_iota(jnp.int32, (ROWS, CAP), 0)
    col = lax.broadcasted_iota(jnp.int32, (ROWS, CAP), 1)
    filled = jnp.int32(0)
    picks = []
    for k in range(BLOCKS):
        source = (shard - k) & (SHARDS - 1)
        block = block_of(routing_ref, source, k)
        count = grids_ref[source, 2 * block] * grids_ref[source, 2 * block + 1]
        picks.append(jnp.where((row == col + filled) & (col < count), 1.0, 0.0))
        filled = filled + count
    pick = jnp.concatenate(picks, axis=1).astype(BF)
    live = lax.broadcasted_iota(jnp.int32, (ROWS, 512), 0) < filled
    total = jnp.zeros((8, ROWS), F32)
    for j in range(4):
        column = pl.multiple_of(((y + j) & 3) * 512, 512)
        value = stay[j][...].astype(F32) + cross[j][...].astype(F32) + bias_ref[pl.ds(column, 512)][None]
        image = jnp.dot(pick, value.astype(BF), preferred_element_type=F32)
        text = text_ref[:, pl.ds(column, 512)]
        value = jnp.where(live, image, text.astype(F32))
        out_ref[:, pl.ds(column, 512)] = value.astype(BF)
        total = total + row_sums(value)
    sum_ref[...] = total


def norm_kernel(emb_ref, s0, s1, s2, s3, gain_ref, *refs):
    out_ref = refs[-1]
    total = s0[...] + s1[...] + s2[...] + s3[...]
    scale = lax.rsqrt(total / D + EPS).T[:, :1]
    out_ref[...] = (emb_ref[...].astype(F32) * scale * gain_ref[...][None]).astype(BF)


def half(width, which):
    return pl.BlockSpec((ROWS, width), lambda i: (which, 0))


def whole(shape):
    return pl.BlockSpec(shape, lambda i: (0,) * len(shape))


def text_half(text):
    _, width = text.shape
    return pl.pallas_call(
        text_kernel,
        grid=(1,),
        in_specs=[half(width, 1)],
        out_specs=[half(width, 1), whole((8, ROWS))],
        out_shape=[jax.ShapeDtypeStruct(text.shape, BF), jax.ShapeDtypeStruct((8, ROWS), F32)],
        name="text_half",
    )(text)


def splice(idx, routing, grids, stay, cross, bias, text, emb):
    _, width = text.shape
    piece = whole((ROWS, 512))
    return pl.pallas_call(
        splice_kernel,
        grid=(1,),
        in_specs=[SMEM] * 3 + [piece] * 8 + [whole((width,)), half(width, 0), ANY],
        out_specs=[half(width, 0), whole((8, ROWS))],
        out_shape=[jax.ShapeDtypeStruct(text.shape, BF), jax.ShapeDtypeStruct((8, ROWS), F32)],
        input_output_aliases={13: 0},
        name="splice",
    )(idx, routing, grids, *stay, *cross, bias, text, emb)


def norm_half(emb, sums, gain, which, base=None):
    _, width = emb.shape
    args = [emb, *sums, gain]
    specs = [half(width, which)] + [whole((8, ROWS))] * 4 + [whole((width,))]
    alias = {}
    if base is not None:
        args.append(base)
        specs.append(ANY)
        alias = {6: 0}
    return pl.pallas_call(
        norm_kernel,
        grid=(1,),
        in_specs=specs,
        out_specs=half(width, which),
        out_shape=jax.ShapeDtypeStruct(emb.shape, BF),
        input_output_aliases=alias,
    )(*args)


def over_tensor(sums):
    across = shift(sums, xh=1)
    return [sums, shift(sums, c=1), across, shift(across, c=1)]


def per_device(
    patches,
    norm_gain,
    norm_bias,
    first_weight,
    first_bias,
    second_weight,
    second_bias,
    text_embeds,
    final_gain,
    image_grids,
    routing,
):
    idx = lax.axis_index(AXES).astype(jnp.int32).reshape(1)
    grids = image_grids.reshape(image_grids.shape[0], -1)

    weights = {(0, 0): second_weight}
    weights[0, 1] = shift(second_weight, xl=1)
    weights[1, 0] = shift(second_weight, z=1)
    weights[3, 0] = shift(second_weight, z=3)
    weights[1, 1] = shift(weights[0, 1], z=1)
    weights[3, 1] = shift(weights[0, 1], z=3)
    weights[2, 0] = shift(weights[1, 0], z=1)
    weights[2, 1] = shift(weights[3, 1], z=3)
    weights = [weights[chunk] for chunk in CHUNKS]

    blocks = first_product(idx, routing, patches, norm_gain, norm_bias, first_weight, first_bias)
    head = {0: blocks[0]}
    tail = {0: jnp.concatenate([shift_dp(blocks[k], k) for k in range(1, BLOCKS)], axis=0)}
    for j in (1, 3, 2):
        head[j] = shift(head[0], y=j)
        tail[j] = shift(tail[0], y=j)

    stay, cross = {}, {}
    for pair in ((1, 3), (2, 0)):
        pieces = [part[j] for j in pair for part in (head, tail)]
        keep, send = second_product(idx, pieces, weights)
        came = shift(send, c=1)
        for side, taken in ((1, cross), (0, stay)):
            for i, j in enumerate(pair):
                at = slice(i * ROWS, (i + 1) * ROWS)
                piece = (keep[side, at].astype(F32) + came[side, at].astype(F32)).astype(BF)
                if side:
                    taken[j] = shift(piece, y=-j % 4, xh=1)
                elif j:
                    taken[j] = shift(piece, y=-j % 4)
                else:
                    taken[j] = piece

    emb, text_sums = text_half(text_embeds)
    normed = norm_half(emb, over_tensor(text_sums), final_gain, 1)
    emb, sums = splice(
        idx, routing, grids, [stay[j] for j in range(4)], [cross[j] for j in range(4)], second_bias, text_embeds, emb
    )
    normed = norm_half(emb, over_tensor(sums), final_gain, 0, normed)
    return (emb, normed)


def solution(mesh):
    mesh = Mesh(mesh.devices.reshape([SIZES[a] for a in AXES]), AXES)
    dp, tensor = ("z", "y", "xl"), ("xh", "c")
    placed = (
        P(dp, None),
        P(),
        P(),
        P(None, tensor),
        P(tensor),
        P(tensor, dp),
        P(tensor),
        P(dp, tensor),
        P(tensor),
        P(),
        P(),
    )
    return jax.shard_map(
        per_device,
        mesh=mesh,
        in_specs=placed,
        out_specs=(P(dp, tensor), P(dp, tensor)),
        check_vma=False,
    )
```

profile of v0, /device:TPU:1, one launch (start us, length us, event | category | flops | bytes accessed | tf_op | source)
XLA Modules:
  0.0 169.1 jit_solution(16274902635830339277)
XLA Ops:
  0.6 2.1 %collective-permute-start.5 = (bf16[1280,256]{1,0:T(8,128)(2,1)}, bf16[1280,256]{1,0:T(8,128)(2,1)S(1)}, u32[]{:S(2)}, u32[]{:S(2)}) collective-permute-start(bf16[1280,256]{1,0:T(8,128)(2,1)} %refs_4_.3), channel_id=1, source_target_pairs={{0,4},{4,0},{1,5},{5,1},{2,6},{6,2},{3,7},{7,3},{8,12},{12,8},{9,1... | collective-permute-start | bytes 1966088 | tf_op jit(solution)/shard_map/ppermute | solution.py:34
  2.7 0.8 copy.19.routing_ref
  3.5 1.7 %copy-done = bf16[1024,1280]{1,0:T(8,128)(2,1)S(1)} copy-done((bf16[1024,1280]{1,0:T(8,128)(2,1)S(1)}, bf16[1024,1280]{1,0:T(8,128)(2,1)}, u32[]{:S(2)}) %copy-start) | copy-done | bytes 2621464
  5.3 0.7 copy-done.3
  5.9 0.7 copy-done.4
  6.6 0.7 copy-done.5
  7.3 11.2 %first_product.1 = (bf16[64,1280]{1,0:T(8,128)(2,1)S(1)}, bf16[64,1280]{1,0:T(8,128)(2,1)S(1)}, bf16[64,1280]{1,0:T(8,128)(2,1)S(1)}, bf16[64,1280]{1,0:T(8,128)(2,1)S(1)}) custom-call(s32[1]{0:T(128)} %bitcast.idx_ref, s32[32,4]{1,0:T(8,128)S(1)} %copy.19.routing_ref, bf16[1024,1280]{1,0:T(8,128)(2,1)S(1)} %copy-done, f32[1280]{0:T(1024)S(1)} %copy-done.3, ...), custom_call_target="tpu_custom_call" | custom-call | tf_op jit(solution)/shard_map/first_product/pallas_call | solution.py:93
  18.6 0.1 collective-permute-start.1
  18.7 1.9 %collective-permute-start.6 = (bf16[1280,256]{1,0:T(8,128)(2,1)S(1)}, bf16[1280,256]{1,0:T(8,128)(2,1)S(1)}, u32[]{:S(2)}, u32[]{:S(2)}) collective-permute-start(bf16[1280,256]{1,0:T(8,128)(2,1)S(1)} %copy-done.1), channel_id=1, source_target_pairs={{0,32},{32,64},{64,96},{96,0},{1,33},{33,65},{65,97},{97,1},{2,34}... | collective-permute-start | bytes 1966088 | tf_op jit(solution)/shard_map/ppermute | solution.py:34
  20.6 1.3 collective-permute-start.2
  21.9 2.9 %collective-permute-start.3 = (bf16[64,1280]{1,0:T(8,128)(2,1)S(1)}, bf16[64,1280]{1,0:T(8,128)(2,1)S(1)}, u32[]{:S(2)}, u32[]{:S(2)}) collective-permute-start(bf16[64,1280]{1,0:T(8,128)(2,1)S(1)} %get-tuple-element.17), channel_id=1, source_target_pairs={{0,12},{4,16},{8,20},{12,24},{16,28},{20,32},{24,36},{28,40},{32,4... | collective-permute-start | bytes 491528 | tf_op jit(solution)/shard_map/ppermute | solution.py:39
  24.8 3.7 %collective-permute-done.1 = bf16[64,1280]{1,0:T(8,128)(2,1)S(1)} collective-permute-done((bf16[64,1280]{1,0:T(8,128)(2,1)S(1)}, bf16[64,1280]{1,0:T(8,128)(2,1)S(1)}, u32[]{:S(2)}, u32[]{:S(2)}) %collective-permute-start.1) | collective-permute-done | bytes 163872 | tf_op jit(solution)/shard_map/ppermute | solution.py:39
  28.5 8.0 %collective-permute-done.2 = bf16[64,1280]{1,0:T(8,128)(2,1)S(1)} collective-permute-done((bf16[64,1280]{1,0:T(8,128)(2,1)S(1)}, bf16[64,1280]{1,0:T(8,128)(2,1)S(1)}, u32[]{:S(2)}, u32[]{:S(2)}) %collective-permute-start.2) | collective-permute-done | bytes 163872 | tf_op jit(solution)/shard_map/ppermute | solution.py:39
  36.6 1.5 collective-permute-start.9
  38.1 0.0 collective-permute-done.3
  38.1 0.1 collective-permute-start.14
  38.2 0.1 collective-permute-start.13
  38.3 2.7 %collective-permute-start.15 = (bf16[64,1280]{1,0:T(8,128)(2,1)S(1)}, bf16[64,1280]{1,0:T(8,128)(2,1)S(1)}, u32[]{:S(2)}, u32[]{:S(2)}) collective-permute-start(bf16[64,1280]{1,0:T(8,128)(2,1)S(1)} %get-tuple-element.14.refs_2_), channel_id=1, source_target_pairs={{0,24},{8,0},{16,8},{24,16},{1,25},{9,1},{17,9},{25,17},{2,26},{10... | collective-permute-start | bytes 491528 | tf_op jit(solution)/shard_map/ppermute | solution.py:34
  41.0 13.6 %collective-permute-done.13.refs_0_ = bf16[64,1280]{1,0:T(8,128)(2,1)S(1)} collective-permute-done((bf16[64,1280]{1,0:T(8,128)(2,1)S(1)}, bf16[64,1280]{1,0:T(8,128)(2,1)S(1)}, u32[]{:S(2)}, u32[]{:S(2)}) %collective-permute-start.13) | collective-permute-done | bytes 163872 | tf_op jit(solution)/shard_map/ppermute | solution.py:34
  54.6 0.0 collective-permute-start.16
  54.6 0.0 collective-permute-done.15.refs_2_
  54.6 1.0 collective-permute-start.11
  55.6 0.0 collective-permute-done.14.refs_1_
  55.6 0.4 collective-permute-start.7
  56.1 0.3 collective-permute-start.8
  56.4 0.0 collective-permute-done.9.refs_11_
  56.4 2.4 %collective-permute-start.10 = (bf16[1280,256]{1,0:T(8,128)(2,1)S(1)}, bf16[1280,256]{1,0:T(8,128)(2,1)S(1)}, u32[]{:S(2)}, u32[]{:S(2)}) collective-permute-start(bf16[1280,256]{1,0:T(8,128)(2,1)S(1)} %collective-permute-done.9.refs_11_), channel_id=1, source_target_pairs={{0,96},{32,0},{64,32},{96,64},{1,97},{33,1},{65,33},{97,65},{2,98}... | collective-permute-start | bytes 1966088 | tf_op jit(solution)/shard_map/ppermute | solution.py:34
  58.7 6.6 %collective-permute-done.16.refs_3_ = bf16[192,1280]{1,0:T(8,128)(2,1)S(1)} collective-permute-done((bf16[192,1280]{1,0:T(8,128)(2,1)S(1)}, bf16[192,1280]{1,0:T(8,128)(2,1)S(1)}, u32[]{:S(2)}, u32[]{:S(2)}) %collective-permute-start.16) | collective-permute-done | bytes 491552 | tf_op jit(solution)/shard_map/ppermute | solution.py:34
  65.4 3.5 %collective-permute-done.11.refs_10_ = bf16[1280,256]{1,0:T(8,128)(2,1)S(1)} collective-permute-done((bf16[1280,256]{1,0:T(8,128)(2,1)S(1)}, bf16[1280,256]{1,0:T(8,128)(2,1)S(1)}, u32[]{:S(2)}, u32[]{:S(2)}) %collective-permute-start.11) | collective-permute-done | bytes 655392 | tf_op jit(solution)/shard_map/ppermute | solution.py:34
  68.9 2.3 %collective-permute-done.7.refs_7_ = bf16[1280,256]{1,0:T(8,128)(2,1)S(1)} collective-permute-done((bf16[1280,256]{1,0:T(8,128)(2,1)S(1)}, bf16[1280,256]{1,0:T(8,128)(2,1)S(1)}, u32[]{:S(2)}, u32[]{:S(2)}) %collective-permute-start.7) | collective-permute-done | bytes 655392 | tf_op jit(solution)/shard_map/ppermute | solution.py:34
  71.1 14.0 %collective-permute-done.8.refs_8_ = bf16[1280,256]{1,0:T(8,128)(2,1)S(1)} collective-permute-done((bf16[1280,256]{1,0:T(8,128)(2,1)S(1)}, bf16[1280,256]{1,0:T(8,128)(2,1)S(1)}, u32[]{:S(2)}, u32[]{:S(2)}) %collective-permute-start.8) | collective-permute-done | bytes 655392 | tf_op jit(solution)/shard_map/ppermute | solution.py:34
  85.2 5.2 %shard_map.123 = (bf16[2,512,512]{2,1,0:T(8,128)(2,1)S(1)}, bf16[2,512,512]{2,1,0:T(8,128)(2,1)}) custom-call(s32[1]{0:T(128)} %bitcast.idx_ref, bf16[64,1280]{1,0:T(8,128)(2,1)S(1)} %collective-permute-done.13.refs_0_, bf16[192,1280]{1,0:T(8,128)(2,1)S(1)} %collective-permute-done.14.refs_1_, bf16[64,1280]{1,0:T(8,128)(2,1)S(1)} %collective-permute-done.15.refs_2_, ...), custom_call_target="tpu_custom_call" | custom-call | tf_op jit(solution)/shard_map/pallas_call | solution.py:143
  90.4 2.8 %collective-permute-start.17 = (bf16[2,512,512]{2,1,0:T(8,128)(2,1)}, bf16[2,512,512]{2,1,0:T(8,128)(2,1)}, u32[]{:S(2)}, u32[]{:S(2)}) collective-permute-start(bf16[2,512,512]{2,1,0:T(8,128)(2,1)} %get-tuple-element.21), channel_id=1, source_target_pairs={{0,1},{1,0},{2,3},{3,2},{4,5},{5,4},{6,7},{7,6},{8,9},{9,8},{10,11... | collective-permute-start | bytes 3145736 | tf_op jit(solution)/shard_map/ppermute | solution.py:34
  93.3 0.9 collective-permute-start
  94.1 6.4 %collective-permute-done.refs_0_ = bf16[64,1280]{1,0:T(8,128)(2,1)S(1)} collective-permute-done((bf16[64,1280]{1,0:T(8,128)(2,1)S(1)}, bf16[64,1280]{1,0:T(8,128)(2,1)S(1)}, u32[]{:S(2)}, u32[]{:S(2)}) %collective-permute-start) | collective-permute-done | bytes 163872 | tf_op jit(solution)/shard_map/ppermute | solution.py:34
  100.5 5.4 %shard_map.122 = (bf16[2,512,512]{2,1,0:T(8,128)(2,1)S(1)}, bf16[2,512,512]{2,1,0:T(8,128)(2,1)}) custom-call(s32[1]{0:T(128)} %bitcast.idx_ref, bf16[64,1280]{1,0:T(8,128)(2,1)S(1)} %collective-permute-done.refs_0_, bf16[192,1280]{1,0:T(8,128)(2,1)S(1)} %collective-permute-done.4.refs_1_, bf16[64,1280]{1,0:T(8,128)(2,1)S(1)} %get-tuple-element.14.refs_2_, ...), custom_call_target="tpu_custom_call" | custom-call | tf_op jit(solution)/shard_map/pallas_call | solution.py:143
  105.9 0.9 collective-permute-start.12
  106.8 3.6 %text_half.1 = (bf16[512,2048]{1,0:T(8,128)(2,1)}, f32[8,256]{1,0:T(8,128)}) custom-call(bf16[512,2048]{1,0:T(8,128)(2,1)} %refs_9_.1), custom_call_target="tpu_custom_call" | custom-call | tf_op jit(solution)/shard_map/text_half/pallas_call | solution.py:210
  110.4 2.5 %collective-permute-start.29 = (f32[8,256]{1,0:T(8,128)}, f32[8,256]{1,0:T(8,128)S(1)}, u32[]{:S(2)}, u32[]{:S(2)}) collective-permute-start(f32[8,256]{1,0:T(8,128)} %get-tuple-element.25.s0), channel_id=1, source_target_pairs={{0,2},{2,0},{1,3},{3,1},{4,6},{6,4},{5,7},{7,5},{8,10},{10,8},{9,1... | collective-permute-start | bytes 24584 | tf_op jit(solution)/shard_map/ppermute | solution.py:34
  112.9 0.3 collective-permute-start.28
  113.2 1.5 collective-permute-done.29.s2
  114.6 1.2 collective-permute-start.30
  115.8 1.5 fusion.7
  117.3 1.0 collective-permute-start.18
  118.2 0.7 collective-permute-start.20
  118.9 4.2 %collective-permute-start.22 = (bf16[256,512]{1,0:T(8,128)(2,1)S(1)}, bf16[256,512]{1,0:T(8,128)(2,1)S(1)}, u32[]{:S(2)}, u32[]{:S(2)}) collective-permute-start(bf16[256,512]{1,0:T(8,128)(2,1)S(1)} %get-tuple-element.27), channel_id=1, source_target_pairs={{0,26},{2,24},{8,2},{10,0},{16,10},{18,8},{24,18},{26,16},{1,27},{... | collective-permute-start | bytes 786440 | tf_op jit(solution)/shard_map/ppermute | solution.py:34
  123.1 2.2 %fusion.6 = (bf16[256,512]{1,0:T(8,128)(2,1)S(1)}, bf16[256,512]{1,0:T(8,128)(2,1)S(1)}, bf16[256,512]{1,0:T(8,128)(2,1)S(1)}, bf16[256,512]{1,0:T(8,128)(2,1)}) fusion(bf16[2,512,512]{2,1,0:T(8,128)(2,1)} %collective-permute-done.12, bf16[2,512,512]{2,1,0:T(8,128)(2,1)S(1)} %get-tuple-element.18), kind=kLoop, calls=%fused_computation.14 | loop fusion | flops 2097152 | bytes 3145728 | tf_op jit(solution)/shard_map/convert_element_type | solution.py:299
  125.3 0.1 collective-permute-start.24
  125.4 0.6 copy-done.15
  126.0 1.4 collective-permute-start.19
  127.3 3.5 %collective-permute-done.18.refs_1_ = bf16[256,512]{1,0:T(8,128)(2,1)S(1)} collective-permute-done((bf16[256,512]{1,0:T(8,128)(2,1)S(1)}, bf16[256,512]{1,0:T(8,128)(2,1)S(1)}, u32[]{:S(2)}, u32[]{:S(2)}) %collective-permute-start.18) | collective-permute-done | bytes 262176 | tf_op jit(solution)/shard_map/ppermute | solution.py:34
  130.8 2.5 %collective-permute-start.21 = (bf16[256,512]{1,0:T(8,128)(2,1)S(1)}, bf16[256,512]{1,0:T(8,128)(2,1)S(1)}, u32[]{:S(2)}, u32[]{:S(2)}) collective-permute-start(bf16[256,512]{1,0:T(8,128)(2,1)S(1)} %get-tuple-element.31), channel_id=1, source_target_pairs={{0,2},{2,0},{8,10},{10,8},{16,18},{18,16},{24,26},{26,24},{1,3},{3... | collective-permute-start | bytes 786440 | tf_op jit(solution)/shard_map/ppermute | solution.py:34
  133.3 6.8 %collective-permute-start.23 = (bf16[256,512]{1,0:T(8,128)(2,1)S(1)}, bf16[256,512]{1,0:T(8,128)(2,1)S(1)}, u32[]{:S(2)}, u32[]{:S(2)}) collective-permute-start(bf16[256,512]{1,0:T(8,128)(2,1)S(1)} %get-tuple-element.30), channel_id=1, source_target_pairs={{0,18},{2,16},{8,26},{10,24},{16,2},{18,0},{24,10},{26,8},{1,19},{... | collective-permute-start | bytes 786440 | tf_op jit(solution)/shard_map/ppermute | solution.py:34
  140.0 1.4 copy.20.grids_ref
  141.4 2.7 %shard_map.124.refs_0_ = bf16[512,2048]{1,0:T(8,128)(2,1)} custom-call(bf16[512,2048]{1,0:T(8,128)(2,1)} %get-tuple-element.22.refs_10_.emb_ref, f32[8,256]{1,0:T(8,128)} %get-tuple-element.25.s0, f32[8,256]{1,0:T(8,128)} %copy-done.14, f32[8,256]{1,0:T(8,128)} %copy-done.13, f32[8,256]{1,0:T(8,128)} %copy-done.15, f32[2048]{0:T(1024)} %gain_ref.5), custom_call_target="tpu_custom_call" | custom-call | tf_op jit(solution)/shard_map/pallas_call | solution.py:243
  144.1 6.9 %collective-permute-done.23.refs_6_ = bf16[256,512]{1,0:T(8,128)(2,1)S(1)} collective-permute-done((bf16[256,512]{1,0:T(8,128)(2,1)S(1)}, bf16[256,512]{1,0:T(8,128)(2,1)S(1)}, u32[]{:S(2)}, u32[]{:S(2)}) %collective-permute-start.23) | collective-permute-done | bytes 262176 | tf_op jit(solution)/shard_map/ppermute | solution.py:34
  151.1 0.7 copy-done.12
  151.7 6.0 %splice.1 = (bf16[512,2048]{1,0:T(8,128)(2,1)}, f32[8,256]{1,0:T(8,128)}) custom-call(s32[1]{0:T(128)} %bitcast.idx_ref, s32[32,4]{1,0:T(8,128)} %copy-done.2, s32[32,8]{1,0:T(8,128)} %copy.20.grids_ref, bf16[256,512]{1,0:T(8,128)(2,1)} %get-tuple-element.33.refs_0_, bf16[256,512]{1,0:T(8,128)(2,1)} %copy-done.6, ...), custom_call_target="tpu_custom_call", output_to_operand_aliasing={{0}: (13, {})} | custom-call | tf_op jit(solution)/shard_map/splice/pallas_call | solution.py:223
  157.8 2.5 %collective-permute-start.26 = (f32[8,256]{1,0:T(8,128)}, f32[8,256]{1,0:T(8,128)S(1)}, u32[]{:S(2)}, u32[]{:S(2)}) collective-permute-start(f32[8,256]{1,0:T(8,128)} %get-tuple-element.24.s0), channel_id=1, source_target_pairs={{0,2},{2,0},{1,3},{3,1},{4,6},{6,4},{5,7},{7,5},{8,10},{10,8},{9,1... | collective-permute-start | bytes 24584 | tf_op jit(solution)/shard_map/ppermute | solution.py:34
  160.2 2.1 %collective-permute-start.25 = (f32[8,256]{1,0:T(8,128)}, f32[8,256]{1,0:T(8,128)S(1)}, u32[]{:S(2)}, u32[]{:S(2)}) collective-permute-start(f32[8,256]{1,0:T(8,128)} %get-tuple-element.24.s0), channel_id=1, source_target_pairs={{0,1},{1,0},{2,3},{3,2},{4,5},{5,4},{6,7},{7,6},{8,9},{9,8},{10,11... | collective-permute-start | bytes 24584 | tf_op jit(solution)/shard_map/ppermute | solution.py:34
  162.4 2.6 %collective-permute-start.27 = (f32[8,256]{1,0:T(8,128)S(1)}, f32[8,256]{1,0:T(8,128)S(1)}, u32[]{:S(2)}, u32[]{:S(2)}) collective-permute-start(f32[8,256]{1,0:T(8,128)S(1)} %collective-permute-done.26.s2), channel_id=1, source_target_pairs={{0,1},{1,0},{2,3},{3,2},{4,5},{5,4},{6,7},{7,6},{8,9},{9,8},{10,11... | collective-permute-start | bytes 24584 | tf_op jit(solution)/shard_map/ppermute | solution.py:34
  165.0 0.8 collective-permute-done.27.s3
  165.8 0.6 copy-done.18
  166.4 2.7 %shard_map.125 = bf16[512,2048]{1,0:T(8,128)(2,1)} custom-call(bf16[512,2048]{1,0:T(8,128)(2,1)} %get-tuple-element.12.emb_ref, f32[8,256]{1,0:T(8,128)} %get-tuple-element.24.s0, f32[8,256]{1,0:T(8,128)} %copy-done.17, f32[8,256]{1,0:T(8,128)} %copy-done.16, f32[8,256]{1,0:T(8,128)} %copy-done.18, f32[2048]{0:T(1024)} %gain_ref.5, ...), custom_call_target="tpu_custom_call", output_to_operand_aliasing={{}: (6, {})} | custom-call | tf_op jit(solution)/shard_map/pallas_call | solution.py:243
  (50 shorter events, 0.1 us)
Async XLA Ops:
  0.6 36.0 %collective-permute-start.5 = (bf16[1280,256]{1,0:T(8,128)(2,1)}, bf16[1280,256]{1,0:T(8,128)(2,1)S(1)}, u32[]{:S(2)}, u32[]{:S(2)}) collective-permute-start(bf16[1280,256]{1,0:T(8,128)(2,1)} %refs_4_.3), channel_id=1, source_target_pairs={{0,4},{4,0},{1,5},{5,1},{2,6},{6,2},{3,7},{7,3},{8,12},{12,8},{9,1... | collective-permute-start | bytes 1966088 | tf_op jit(solution)/shard_map/ppermute | solution.py:34
  3.5 15.1 %copy-start.2 = (s32[32,4]{1,0:T(8,128)}, s32[32,4]{1,0:T(8,128)S(1)}, u32[]{:S(2)}) copy-start(s32[32,4]{1,0:T(8,128)S(1)} %copy.19.routing_ref) | copy-start | bytes 1540
  3.5 1.7 %copy-start = (bf16[1024,1280]{1,0:T(8,128)(2,1)S(1)}, bf16[1024,1280]{1,0:T(8,128)(2,1)}, u32[]{:S(2)}) copy-start(bf16[1024,1280]{1,0:T(8,128)(2,1)} %patches_ref.1) | copy-start | bytes 7864324
  5.2 0.7 copy-start.3
  5.9 0.7 copy-start.4
  6.6 0.7 copy-start.5
  7.3 11.4 %copy-start.1 = (bf16[1280,256]{1,0:T(8,128)(2,1)S(1)}, bf16[1280,256]{1,0:T(8,128)(2,1)}, u32[]{:S(2)}) copy-start(bf16[1280,256]{1,0:T(8,128)(2,1)} %refs_4_.3) | copy-start | bytes 1966084
  18.6 9.9 %collective-permute-start.1 = (bf16[64,1280]{1,0:T(8,128)(2,1)S(1)}, bf16[64,1280]{1,0:T(8,128)(2,1)S(1)}, u32[]{:S(2)}, u32[]{:S(2)}) collective-permute-start(bf16[64,1280]{1,0:T(8,128)(2,1)S(1)} %get-tuple-element.15), channel_id=1, source_target_pairs={{0,4},{4,8},{8,12},{12,16},{16,20},{20,24},{24,28},{28,32},{32,36}... | collective-permute-start | bytes 491528 | tf_op jit(solution)/shard_map/ppermute | solution.py:39
  18.7 37.4 %collective-permute-start.6 = (bf16[1280,256]{1,0:T(8,128)(2,1)S(1)}, bf16[1280,256]{1,0:T(8,128)(2,1)S(1)}, u32[]{:S(2)}, u32[]{:S(2)}) collective-permute-start(bf16[1280,256]{1,0:T(8,128)(2,1)S(1)} %copy-done.1), channel_id=1, source_target_pairs={{0,32},{32,64},{64,96},{96,0},{1,33},{33,65},{65,97},{97,1},{2,34}... | collective-permute-start | bytes 1966088 | tf_op jit(solution)/shard_map/ppermute | solution.py:34
  20.6 16.0 %collective-permute-start.2 = (bf16[64,1280]{1,0:T(8,128)(2,1)S(1)}, bf16[64,1280]{1,0:T(8,128)(2,1)S(1)}, u32[]{:S(2)}, u32[]{:S(2)}) collective-permute-start(bf16[64,1280]{1,0:T(8,128)(2,1)S(1)} %get-tuple-element.16), channel_id=1, source_target_pairs={{0,8},{4,12},{8,16},{12,20},{16,24},{20,28},{24,32},{28,36},{32,40... | collective-permute-start | bytes 491528 | tf_op jit(solution)/shard_map/ppermute | solution.py:39
  21.9 16.3 %collective-permute-start.3 = (bf16[64,1280]{1,0:T(8,128)(2,1)S(1)}, bf16[64,1280]{1,0:T(8,128)(2,1)S(1)}, u32[]{:S(2)}, u32[]{:S(2)}) collective-permute-start(bf16[64,1280]{1,0:T(8,128)(2,1)S(1)} %get-tuple-element.17), channel_id=1, source_target_pairs={{0,12},{4,16},{8,20},{12,24},{16,28},{20,32},{24,36},{28,40},{32,4... | collective-permute-start | bytes 491528 | tf_op jit(solution)/shard_map/ppermute | solution.py:39
  36.6 19.8 %collective-permute-start.9 = (bf16[1280,256]{1,0:T(8,128)(2,1)S(1)}, bf16[1280,256]{1,0:T(8,128)(2,1)S(1)}, u32[]{:S(2)}, u32[]{:S(2)}) collective-permute-start(bf16[1280,256]{1,0:T(8,128)(2,1)S(1)} %collective-permute-done.5.refs_5_), channel_id=1, source_target_pairs={{0,96},{32,0},{64,32},{96,64},{1,97},{33,1},{65,33},{97,65},{2,98}... | collective-permute-start | bytes 1966088 | tf_op jit(solution)/shard_map/ppermute | solution.py:34
  38.1 17.5 %collective-permute-start.14 = (bf16[192,1280]{1,0:T(8,128)(2,1)S(1)}, bf16[192,1280]{1,0:T(8,128)(2,1)S(1)}, u32[]{:S(2)}, u32[]{:S(2)}) collective-permute-start(bf16[192,1280]{1,0:T(8,128)(2,1)S(1)} %constant_dynamic-update-slice_fusion.refs_3_), channel_id=1, source_target_pairs={{0,8},{8,16},{16,24},{24,0},{1,9},{9,17},{17,25},{25,1},{2,10},{10... | collective-permute-start | bytes 1474568 | tf_op jit(solution)/shard_map/ppermute | solution.py:34
  38.2 16.4 %collective-permute-start.13 = (bf16[64,1280]{1,0:T(8,128)(2,1)S(1)}, bf16[64,1280]{1,0:T(8,128)(2,1)S(1)}, u32[]{:S(2)}, u32[]{:S(2)}) collective-permute-start(bf16[64,1280]{1,0:T(8,128)(2,1)S(1)} %get-tuple-element.14.refs_2_), channel_id=1, source_target_pairs={{0,8},{8,16},{16,24},{24,0},{1,9},{9,17},{17,25},{25,1},{2,10},{10... | collective-permute-start | bytes 491528 | tf_op jit(solution)/shard_map/ppermute | solution.py:34
  38.3 16.3 %collective-permute-start.15 = (bf16[64,1280]{1,0:T(8,128)(2,1)S(1)}, bf16[64,1280]{1,0:T(8,128)(2,1)S(1)}, u32[]{:S(2)}, u32[]{:S(2)}) collective-permute-start(bf16[64,1280]{1,0:T(8,128)(2,1)S(1)} %get-tuple-element.14.refs_2_), channel_id=1, source_target_pairs={{0,24},{8,0},{16,8},{24,16},{1,25},{9,1},{17,9},{25,17},{2,26},{10... | collective-permute-start | bytes 491528 | tf_op jit(solution)/shard_map/ppermute | solution.py:34
  54.6 10.8 %collective-permute-start.16 = (bf16[192,1280]{1,0:T(8,128)(2,1)S(1)}, bf16[192,1280]{1,0:T(8,128)(2,1)S(1)}, u32[]{:S(2)}, u32[]{:S(2)}) collective-permute-start(bf16[192,1280]{1,0:T(8,128)(2,1)S(1)} %constant_dynamic-update-slice_fusion.refs_3_), channel_id=1, source_target_pairs={{0,24},{8,0},{16,8},{24,16},{1,25},{9,1},{17,9},{25,17},{2,26},{10... | collective-permute-start | bytes 1474568 | tf_op jit(solution)/shard_map/ppermute | solution.py:34
  54.6 14.3 %collective-permute-start.11 = (bf16[1280,256]{1,0:T(8,128)(2,1)S(1)}, bf16[1280,256]{1,0:T(8,128)(2,1)S(1)}, u32[]{:S(2)}, u32[]{:S(2)}) collective-permute-start(bf16[1280,256]{1,0:T(8,128)(2,1)S(1)} %copy-done.1), channel_id=1, source_target_pairs={{0,96},{32,0},{64,32},{96,64},{1,97},{33,1},{65,33},{97,65},{2,98}... | collective-permute-start | bytes 1966088 | tf_op jit(solution)/shard_map/ppermute | solution.py:34
  55.6 15.5 %collective-permute-start.7 = (bf16[1280,256]{1,0:T(8,128)(2,1)S(1)}, bf16[1280,256]{1,0:T(8,128)(2,1)S(1)}, u32[]{:S(2)}, u32[]{:S(2)}) collective-permute-start(bf16[1280,256]{1,0:T(8,128)(2,1)S(1)} %collective-permute-done.5.refs_5_), channel_id=1, source_target_pairs={{0,32},{32,64},{64,96},{96,0},{1,33},{33,65},{65,97},{97,1},{2,34}... | collective-permute-start | bytes 1966088 | tf_op jit(solution)/shard_map/ppermute | solution.py:34
  56.1 29.1 %collective-permute-start.8 = (bf16[1280,256]{1,0:T(8,128)(2,1)S(1)}, bf16[1280,256]{1,0:T(8,128)(2,1)S(1)}, u32[]{:S(2)}, u32[]{:S(2)}) collective-permute-start(bf16[1280,256]{1,0:T(8,128)(2,1)S(1)} %collective-permute-done.6.refs_6_), channel_id=1, source_target_pairs={{0,32},{32,64},{64,96},{96,0},{1,33},{33,65},{65,97},{97,1},{2,34}... | collective-permute-start | bytes 1966088 | tf_op jit(solution)/shard_map/ppermute | solution.py:34
  56.4 28.8 %collective-permute-start.10 = (bf16[1280,256]{1,0:T(8,128)(2,1)S(1)}, bf16[1280,256]{1,0:T(8,128)(2,1)S(1)}, u32[]{:S(2)}, u32[]{:S(2)}) collective-permute-start(bf16[1280,256]{1,0:T(8,128)(2,1)S(1)} %collective-permute-done.9.refs_11_), channel_id=1, source_target_pairs={{0,96},{32,0},{64,32},{96,64},{1,97},{33,1},{65,33},{97,65},{2,98}... | collective-permute-start | bytes 1966088 | tf_op jit(solution)/shard_map/ppermute | solution.py:34
  65.4 35.2 %collective-permute-start.4 = (bf16[192,1280]{1,0:T(8,128)(2,1)S(1)}, bf16[192,1280]{1,0:T(8,128)(2,1)S(1)}, u32[]{:S(2)}, u32[]{:S(2)}) collective-permute-start(bf16[192,1280]{1,0:T(8,128)(2,1)S(1)} %constant_dynamic-update-slice_fusion.refs_3_), channel_id=1, source_target_pairs={{0,16},{8,24},{16,0},{24,8},{1,17},{9,25},{17,1},{25,9},{2,18},{10... | collective-permute-start | bytes 1474568 | tf_op jit(solution)/shard_map/ppermute | solution.py:34
  90.4 25.4 %collective-permute-start.17 = (bf16[2,512,512]{2,1,0:T(8,128)(2,1)}, bf16[2,512,512]{2,1,0:T(8,128)(2,1)}, u32[]{:S(2)}, u32[]{:S(2)}) collective-permute-start(bf16[2,512,512]{2,1,0:T(8,128)(2,1)} %get-tuple-element.21), channel_id=1, source_target_pairs={{0,1},{1,0},{2,3},{3,2},{4,5},{5,4},{6,7},{7,6},{8,9},{9,8},{10,11... | collective-permute-start | bytes 3145736 | tf_op jit(solution)/shard_map/ppermute | solution.py:34
  93.3 7.3 %collective-permute-start = (bf16[64,1280]{1,0:T(8,128)(2,1)S(1)}, bf16[64,1280]{1,0:T(8,128)(2,1)S(1)}, u32[]{:S(2)}, u32[]{:S(2)}) collective-permute-start(bf16[64,1280]{1,0:T(8,128)(2,1)S(1)} %get-tuple-element.14.refs_2_), channel_id=1, source_target_pairs={{0,16},{8,24},{16,0},{24,8},{1,17},{9,25},{17,1},{25,9},{2,18},{10... | collective-permute-start | bytes 491528 | tf_op jit(solution)/shard_map/ppermute | solution.py:34
  105.9 12.9 %collective-permute-start.12 = (bf16[2,512,512]{2,1,0:T(8,128)(2,1)}, bf16[2,512,512]{2,1,0:T(8,128)(2,1)}, u32[]{:S(2)}, u32[]{:S(2)}) collective-permute-start(bf16[2,512,512]{2,1,0:T(8,128)(2,1)} %get-tuple-element.19), channel_id=1, source_target_pairs={{0,1},{1,0},{2,3},{3,2},{4,5},{5,4},{6,7},{7,6},{8,9},{9,8},{10,11... | collective-permute-start | bytes 3145736 | tf_op jit(solution)/shard_map/ppermute | solution.py:34
  110.4 4.2 %collective-permute-start.29 = (f32[8,256]{1,0:T(8,128)}, f32[8,256]{1,0:T(8,128)S(1)}, u32[]{:S(2)}, u32[]{:S(2)}) collective-permute-start(f32[8,256]{1,0:T(8,128)} %get-tuple-element.25.s0), channel_id=1, source_target_pairs={{0,2},{2,0},{1,3},{3,1},{4,6},{6,4},{5,7},{7,5},{8,10},{10,8},{9,1... | collective-permute-start | bytes 24584 | tf_op jit(solution)/shard_map/ppermute | solution.py:34
  112.9 12.4 %collective-permute-start.28 = (f32[8,256]{1,0:T(8,128)}, f32[8,256]{1,0:T(8,128)S(1)}, u32[]{:S(2)}, u32[]{:S(2)}) collective-permute-start(f32[8,256]{1,0:T(8,128)} %get-tuple-element.25.s0), channel_id=1, source_target_pairs={{0,1},{1,0},{2,3},{3,2},{4,5},{5,4},{6,7},{7,6},{8,9},{9,8},{10,11... | collective-permute-start | bytes 24584 | tf_op jit(solution)/shard_map/ppermute | solution.py:34
  114.6 10.6 %copy-start.13 = (f32[8,256]{1,0:T(8,128)}, f32[8,256]{1,0:T(8,128)S(1)}, u32[]{:S(2)}) copy-start(f32[8,256]{1,0:T(8,128)S(1)} %collective-permute-done.29.s2) | copy-start | bytes 24580
  114.6 10.7 %collective-permute-start.30 = (f32[8,256]{1,0:T(8,128)S(1)}, f32[8,256]{1,0:T(8,128)S(1)}, u32[]{:S(2)}, u32[]{:S(2)}) collective-permute-start(f32[8,256]{1,0:T(8,128)S(1)} %collective-permute-done.29.s2), channel_id=1, source_target_pairs={{0,1},{1,0},{2,3},{3,2},{4,5},{5,4},{6,7},{7,6},{8,9},{9,8},{10,11... | collective-permute-start | bytes 24584 | tf_op jit(solution)/shard_map/ppermute | solution.py:34
  117.3 13.6 %collective-permute-start.18 = (bf16[256,512]{1,0:T(8,128)(2,1)S(1)}, bf16[256,512]{1,0:T(8,128)(2,1)S(1)}, u32[]{:S(2)}, u32[]{:S(2)}) collective-permute-start(bf16[256,512]{1,0:T(8,128)(2,1)S(1)} %get-tuple-element.29), channel_id=1, source_target_pairs={{0,24},{8,0},{16,8},{24,16},{1,25},{9,1},{17,9},{25,17},{2,26},{10... | collective-permute-start | bytes 786440 | tf_op jit(solution)/shard_map/ppermute | solution.py:34
  118.2 15.1 %collective-permute-start.20 = (bf16[256,512]{1,0:T(8,128)(2,1)S(1)}, bf16[256,512]{1,0:T(8,128)(2,1)S(1)}, u32[]{:S(2)}, u32[]{:S(2)}) collective-permute-start(bf16[256,512]{1,0:T(8,128)(2,1)S(1)} %get-tuple-element.28), channel_id=1, source_target_pairs={{0,8},{8,16},{16,24},{24,0},{1,9},{9,17},{17,25},{25,1},{2,10},{10... | collective-permute-start | bytes 786440 | tf_op jit(solution)/shard_map/ppermute | solution.py:34
  118.9 25.2 %collective-permute-start.22 = (bf16[256,512]{1,0:T(8,128)(2,1)S(1)}, bf16[256,512]{1,0:T(8,128)(2,1)S(1)}, u32[]{:S(2)}, u32[]{:S(2)}) collective-permute-start(bf16[256,512]{1,0:T(8,128)(2,1)S(1)} %get-tuple-element.27), channel_id=1, source_target_pairs={{0,26},{2,24},{8,2},{10,0},{16,10},{18,8},{24,18},{26,16},{1,27},{... | collective-permute-start | bytes 786440 | tf_op jit(solution)/shard_map/ppermute | solution.py:34
  125.3 16.1 %copy-start.14 = (f32[8,256]{1,0:T(8,128)}, f32[8,256]{1,0:T(8,128)S(1)}, u32[]{:S(2)}) copy-start(f32[8,256]{1,0:T(8,128)S(1)} %collective-permute-done.28.s1) | copy-start | bytes 24580
  125.3 18.8 %collective-permute-start.24 = (bf16[256,512]{1,0:T(8,128)(2,1)S(1)}, bf16[256,512]{1,0:T(8,128)(2,1)S(1)}, u32[]{:S(2)}, u32[]{:S(2)}) collective-permute-start(bf16[256,512]{1,0:T(8,128)(2,1)S(1)} %get-tuple-element.26), channel_id=1, source_target_pairs={{0,10},{2,8},{8,18},{10,16},{16,26},{18,24},{24,2},{26,0},{1,11},{... | collective-permute-start | bytes 786440 | tf_op jit(solution)/shard_map/ppermute | solution.py:34
  125.4 0.6 copy-start.15
  126.0 18.1 %collective-permute-start.19 = (bf16[256,512]{1,0:T(8,128)(2,1)S(1)}, bf16[256,512]{1,0:T(8,128)(2,1)S(1)}, u32[]{:S(2)}, u32[]{:S(2)}) collective-permute-start(bf16[256,512]{1,0:T(8,128)(2,1)S(1)} %get-tuple-element.32), channel_id=1, source_target_pairs={{0,16},{8,24},{16,0},{24,8},{1,17},{9,25},{17,1},{25,9},{2,18},{10... | collective-permute-start | bytes 786440 | tf_op jit(solution)/shard_map/ppermute | solution.py:34
  130.8 13.2 %copy-start.6 = (bf16[256,512]{1,0:T(8,128)(2,1)}, bf16[256,512]{1,0:T(8,128)(2,1)S(1)}, u32[]{:S(2)}) copy-start(bf16[256,512]{1,0:T(8,128)(2,1)S(1)} %collective-permute-done.18.refs_1_) | copy-start | bytes 786436
  130.8 13.3 %collective-permute-start.21 = (bf16[256,512]{1,0:T(8,128)(2,1)S(1)}, bf16[256,512]{1,0:T(8,128)(2,1)S(1)}, u32[]{:S(2)}, u32[]{:S(2)}) collective-permute-start(bf16[256,512]{1,0:T(8,128)(2,1)S(1)} %get-tuple-element.31), channel_id=1, source_target_pairs={{0,2},{2,0},{8,10},{10,8},{16,18},{18,16},{24,26},{26,24},{1,3},{3... | collective-permute-start | bytes 786440 | tf_op jit(solution)/shard_map/ppermute | solution.py:34
  133.3 10.8 %copy-start.7 = (bf16[256,512]{1,0:T(8,128)(2,1)}, bf16[256,512]{1,0:T(8,128)(2,1)S(1)}, u32[]{:S(2)}) copy-start(bf16[256,512]{1,0:T(8,128)(2,1)S(1)} %collective-permute-done.20.refs_3_) | copy-start | bytes 786436
  133.3 17.8 %collective-permute-start.23 = (bf16[256,512]{1,0:T(8,128)(2,1)S(1)}, bf16[256,512]{1,0:T(8,128)(2,1)S(1)}, u32[]{:S(2)}, u32[]{:S(2)}) collective-permute-start(bf16[256,512]{1,0:T(8,128)(2,1)S(1)} %get-tuple-element.30), channel_id=1, source_target_pairs={{0,18},{2,16},{8,26},{10,24},{16,2},{18,0},{24,10},{26,8},{1,19},{... | collective-permute-start | bytes 786440 | tf_op jit(solution)/shard_map/ppermute | solution.py:34
  144.1 7.0 %copy-start.8 = (bf16[256,512]{1,0:T(8,128)(2,1)}, bf16[256,512]{1,0:T(8,128)(2,1)S(1)}, u32[]{:S(2)}) copy-start(bf16[256,512]{1,0:T(8,128)(2,1)S(1)} %collective-permute-done.22.refs_5_) | copy-start | bytes 786436
  144.1 7.0 %copy-start.9 = (bf16[256,512]{1,0:T(8,128)(2,1)}, bf16[256,512]{1,0:T(8,128)(2,1)S(1)}, u32[]{:S(2)}) copy-start(bf16[256,512]{1,0:T(8,128)(2,1)S(1)} %collective-permute-done.24.refs_7_) | copy-start | bytes 786436
  144.1 6.9 %copy-start.10 = (bf16[256,512]{1,0:T(8,128)(2,1)}, bf16[256,512]{1,0:T(8,128)(2,1)S(1)}, u32[]{:S(2)}) copy-start(bf16[256,512]{1,0:T(8,128)(2,1)S(1)} %collective-permute-done.19.refs_2_) | copy-start | bytes 786436
  144.1 6.9 %copy-start.11 = (bf16[256,512]{1,0:T(8,128)(2,1)}, bf16[256,512]{1,0:T(8,128)(2,1)S(1)}, u32[]{:S(2)}) copy-start(bf16[256,512]{1,0:T(8,128)(2,1)S(1)} %collective-permute-done.21.refs_4_) | copy-start | bytes 786436
  151.0 0.7 copy-start.12
  157.8 4.6 %collective-permute-start.26 = (f32[8,256]{1,0:T(8,128)}, f32[8,256]{1,0:T(8,128)S(1)}, u32[]{:S(2)}, u32[]{:S(2)}) collective-permute-start(f32[8,256]{1,0:T(8,128)} %get-tuple-element.24.s0), channel_id=1, source_target_pairs={{0,2},{2,0},{1,3},{3,1},{4,6},{6,4},{5,7},{7,5},{8,10},{10,8},{9,1... | collective-permute-start | bytes 24584 | tf_op jit(solution)/shard_map/ppermute | solution.py:34
  160.2 4.8 %collective-permute-start.25 = (f32[8,256]{1,0:T(8,128)}, f32[8,256]{1,0:T(8,128)S(1)}, u32[]{:S(2)}, u32[]{:S(2)}) collective-permute-start(f32[8,256]{1,0:T(8,128)} %get-tuple-element.24.s0), channel_id=1, source_target_pairs={{0,1},{1,0},{2,3},{3,2},{4,5},{5,4},{6,7},{7,6},{8,9},{9,8},{10,11... | collective-permute-start | bytes 24584 | tf_op jit(solution)/shard_map/ppermute | solution.py:34
  162.4 3.5 %copy-start.16 = (f32[8,256]{1,0:T(8,128)}, f32[8,256]{1,0:T(8,128)S(1)}, u32[]{:S(2)}) copy-start(f32[8,256]{1,0:T(8,128)S(1)} %collective-permute-done.26.s2) | copy-start | bytes 24580
  162.4 3.5 %collective-permute-start.27 = (f32[8,256]{1,0:T(8,128)S(1)}, f32[8,256]{1,0:T(8,128)S(1)}, u32[]{:S(2)}, u32[]{:S(2)}) collective-permute-start(f32[8,256]{1,0:T(8,128)S(1)} %collective-permute-done.26.s2), channel_id=1, source_target_pairs={{0,1},{1,0},{2,3},{3,2},{4,5},{5,4},{6,7},{7,6},{8,9},{9,8},{10,11... | collective-permute-start | bytes 24584 | tf_op jit(solution)/shard_map/ppermute | solution.py:34
  165.0 0.8 copy-start.17
  165.8 0.6 copy-start.18
where the time goes:
time: 170 us; the launch traced here: 169 us
  waiting for transfers between devices  70.9 us (42%)
  starting transfers between devices  48.9 us (29%)
  Pallas kernels  36.9 us (22%)
  local copies, waits for them, and re-layouts  7.89 us (5%)
  other arithmetic  3.66 us (2%)
    ppermute x28, waiting for transfers between devices, shift(): return lax.ppermute(value, axes, pairs)  59.2 us
    ppermute x28, starting transfers between devices, shift(): return lax.ppermute(value, axes, pairs)  44.6 us
    ppermute x3, waiting for transfers between devices, shift_dp(): return lax.ppermute(value, ('z', 'y', 'xl'), pairs)  11.8 us
    pallas_call x1, Pallas kernels, first_product(): pl.pallas_call(first_kernel, grid=(width // cut,), in_specs=[SMEM, SMEM,...  11.2 us
    pallas_call x2, Pallas kernels, second_product(): pl.pallas_call(second_kernel, in_specs=[SMEM] + [VMEM] * 12, out_specs=[V...  10.7 us
    unnamed x41, local copies, waits for them, and re-layouts  6.52 us
    pallas_call x1, Pallas kernels, splice(): pl.pallas_call(splice_kernel, grid=(1,), in_specs=[SMEM] * 3 + [piece] *...  6.02 us
    pallas_call x2, Pallas kernels, norm_half(): pl.pallas_call(norm_kernel, grid=(1,), in_specs=specs, out_specs=half(wid...  5.33 us
  transfers between devices with their start and end apart: 31, of which 12 were waited for; matrix products, arithmetic and copies ran while one was open for 3% of the time, Pallas kernels for 17%

commit v1 on v0

v1 whole, which is shorter than its diff:
```python
import itertools

import jax
import jax.numpy as jnp
import numpy as np
from jax import lax
from jax.experimental import pallas as pl
from jax.experimental.pallas import tpu as pltpu
from jax.sharding import Mesh, PartitionSpec as P


D = 8192
EPS = 1e-06
AXES = ("z", "y", "xl", "xh", "c")
SIZES = {"z": 4, "y": 4, "xl": 2, "xh": 2, "c": 2}
SHARDS = 32
BLOCKS = 4
CAP = 64
ROWS = BLOCKS * CAP
BF = jnp.bfloat16
F32 = jnp.float32
VMEM = pl.BlockSpec(memory_space=pltpu.VMEM)
SMEM = pl.BlockSpec(memory_space=pltpu.SMEM)
ANY = pl.BlockSpec(memory_space=pl.ANY)


def shift(value, **deltas):
    axes = tuple(a for a in AXES if a in deltas)
    sizes = [SIZES[a] for a in axes]
    pairs = []
    for src in itertools.product(*[range(s) for s in sizes]):
        dst = [(i + deltas[a]) % s for i, a, s in zip(src, axes, sizes)]
        pairs.append((int(np.ravel_multi_index(src, sizes)), int(np.ravel_multi_index(dst, sizes))))
    return lax.ppermute(value, axes, pairs)


def shift_dp(value, distance):
    pairs = [(i, (i + distance) % SHARDS) for i in range(SHARDS)]
    return lax.ppermute(value, ("z", "y", "xl"), pairs)


def place(idx_ref):
    i = idx_ref[0]
    return i >> 5, (i >> 3) & 3, (i >> 2) & 1, (i >> 1) & 1, i & 1, i >> 2


def block_of(routing_ref, shard, offset):
    block = jnp.int32(0)
    for b in range(1, BLOCKS):
        block = jnp.where(routing_ref[b, shard] == offset, b, block)
    return block


def first_kernel(idx_ref, routing_ref, patches_ref, gain_hbm, bias_hbm, w_hbm, b_hbm, *refs):
    outs = refs[:BLOCKS]
    raw, scr, merged, wide, acc, gain_ref, bias_ref, b_ref, sems = refs[BLOCKS:]
    shard = place(idx_ref)[5]
    width = patches_ref.shape[1]
    tiles = width // 128
    cuts = [slice(n, n + 256) for n in range(0, w_hbm.shape[1], 256)]

    copies = []
    for small, held in ((gain_hbm, gain_ref), (bias_hbm, bias_ref)):
        copies.append(pltpu.make_async_copy(small, held, sems.at[len(copies)]))
    for k in range(BLOCKS):
        rows = pl.ds(pl.multiple_of(block_of(routing_ref, shard, k) * ROWS, ROWS), ROWS)
        copies.append(pltpu.make_async_copy(patches_ref.at[rows, :], raw.at[k], sems.at[len(copies)]))
    for j in range(4):
        copies.append(pltpu.make_async_copy(w_hbm.at[pl.ds(j * width, width), :], wide.at[j], sems.at[len(copies)]))
    copies.append(pltpu.make_async_copy(b_hbm, b_ref, sems.at[len(copies)]))
    for copy in copies:
        copy.start()
    for copy in copies[:2]:
        copy.wait()
    for k in range(BLOCKS):
        copies[2 + k].wait()
        for t in range(tiles):
            scr[k, t] = raw[k, :, t * 128 : (t + 1) * 128].astype(F32)

    def normalize(j):
        for k in range(BLOCKS):
            for half in range(2):
                x = [scr[k, t, pl.ds(j + 128 * half, 32, stride=4), :] for t in range(tiles)]
                mean = jnp.sum(sum(x), axis=-1, keepdims=True) / width
                x = [v - mean for v in x]
                variance = jnp.sum(sum(v * v for v in x), axis=-1, keepdims=True) / width
                scale = lax.rsqrt(variance + EPS)
                at = slice(k * CAP + half * 32, k * CAP + half * 32 + 32)
                for t, v in enumerate(x):
                    lanes = slice(t * 128, (t + 1) * 128)
                    merged[j, at, lanes] = (v * scale * gain_ref[lanes][None] + bias_ref[lanes][None]).astype(BF)

    normalize(0)
    for j in range(4):
        copies[2 + BLOCKS + j].wait()
        if j < 3:
            normalize(j + 1)
        else:
            copies[-1].wait()
        for cut in cuts:
            part = jnp.dot(merged[j], wide[j, :, cut], preferred_element_type=F32)
            if j == 0:
                acc[:, cut] = part
            elif j < 3:
                acc[:, cut] += part
            else:
                h = acc[:, cut] + part + b_ref[cut][None]
                h = (0.5 * h * (1.0 + lax.erf(h * np.float32(np.sqrt(0.5))))).astype(BF)
                for k, o in enumerate(outs):
                    o[:, cut] = h[k * CAP : (k + 1) * CAP, :]


def first_product(idx, routing, patches, gain, bias, weight, bias1):
    _, width = weight.shape
    vit = patches.shape[1]
    return pl.pallas_call(
        first_kernel,
        in_specs=[SMEM, SMEM] + [ANY] * 5,
        out_specs=[VMEM] * BLOCKS,
        out_shape=[jax.ShapeDtypeStruct((CAP, width), BF)] * BLOCKS,
        scratch_shapes=[
            pltpu.VMEM((BLOCKS, ROWS, vit), BF),
            pltpu.VMEM((BLOCKS, vit // 128, ROWS, 128), F32),
            pltpu.VMEM((4, ROWS, vit), BF),
            pltpu.VMEM((4, vit, width), BF),
            pltpu.VMEM((ROWS, width), F32),
            pltpu.VMEM(gain.shape, F32),
            pltpu.VMEM(bias.shape, F32),
            pltpu.VMEM(bias1.shape, F32),
            pltpu.SemaphoreType.DMA((7 + BLOCKS,)),
        ],
        compiler_params=pltpu.CompilerParams(vmem_limit_bytes=48 << 20),
        name="first_product",
    )(idx, routing, patches, gain, bias, weight, bias1)


CHUNKS = tuple((dz, dx) for dz in range(4) for dx in range(2))


def each_chunk(idx_ref, weights, wanted, use):
    z, _, xl, xh, c, _ = place(idx_ref)
    for (dz, dx), w in zip(CHUNKS, weights):
        group = (z - dz) & 3
        column = pl.ds(pl.multiple_of((xl ^ dx) * 256, 256), 256)
        side = (group >> 1) ^ xh

        @pl.when((group & 1) ^ c == wanted)
        def _():
            use(side, column, w)


def product(rows, i, w):
    return jnp.dot(rows[i * ROWS : (i + 1) * ROWS, :], w[...], preferred_element_type=F32)


def send_kernel(idx_ref, *refs):
    pieces = refs[:4]
    send, rows = refs[12:]
    for i in range(2):
        rows[i * ROWS : i * ROWS + CAP, :] = pieces[2 * i][...]
        rows[i * ROWS + CAP : (i + 1) * ROWS, :] = pieces[2 * i + 1][...]

    def use(side, column, w):
        for i in range(2):
            send[side, i * ROWS : (i + 1) * ROWS, column] = product(rows, i, w).astype(BF)

    each_chunk(idx_ref, refs[4:12], 1, use)


def keep_kernel(idx_ref, rows, came, *refs):
    outs = refs[8:]
    split = len(outs) == 4

    def use(side, column, w):
        values = []
        for i in range(2):
            at = slice(i * ROWS, (i + 1) * ROWS)
            values.append((product(rows, i, w) + came[side, at, column].astype(F32)).astype(BF))
        for s in range(2):

            @pl.when(side == s)
            def _():
                for i, v in enumerate(values):
                    if split:
                        outs[2 * s + i][:, column] = v
                    else:
                        outs[s][i * ROWS : (i + 1) * ROWS, column] = v

    each_chunk(idx_ref, refs[:8], 0, use)


def send_product(idx, pieces, weights):
    depth = weights[0].shape[0]
    return pl.pallas_call(
        send_kernel,
        in_specs=[SMEM] + [VMEM] * 12,
        out_specs=[VMEM, VMEM],
        out_shape=[jax.ShapeDtypeStruct((2, 2 * ROWS, 512), BF), jax.ShapeDtypeStruct((2 * ROWS, depth), BF)],
        compiler_params=pltpu.CompilerParams(vmem_limit_bytes=40 << 20),
    )(idx, *pieces, *weights)


def keep_product(idx, rows, came, weights, split):
    height, number = (ROWS, 4) if split else (2 * ROWS, 2)
    return pl.pallas_call(
        keep_kernel,
        in_specs=[SMEM] + [VMEM] * 10,
        out_specs=[VMEM] * number,
        out_shape=[jax.ShapeDtypeStruct((height, 512), BF)] * number,
        compiler_params=pltpu.CompilerParams(vmem_limit_bytes=40 << 20),
    )(idx, rows, came, *weights)


def lane_sums(v):
    v = v * v
    return sum(v[:, i : i + 128] for i in range(0, v.shape[1], 128))


def row_sums(v):
    ones = jnp.ones((8, v.shape[1]), F32)
    return lax.dot_general(ones, v, (((1,), (1,)), ((), ())), precision=lax.Precision.HIGHEST, preferred_element_type=F32)


def text_kernel(text_ref, out_ref, sum_ref):
    value = text_ref[...]
    out_ref[...] = value
    sum_ref[...] = row_sums(lane_sums(value.astype(F32)))


def splice_kernel(idx_ref, routing_ref, grids_ref, *refs):
    pieces = [[refs[0], refs[1]], [refs[2]], [refs[3], refs[4]], [refs[5]]]
    bias_ref, text_ref, _, out_ref, sum_ref = refs[6:]
    _, y, _, _, _, shard = place(idx_ref)
    row = lax.broadcasted_iota(jnp.int32, (ROWS, CAP), 0)
    col = lax.broadcasted_iota(jnp.int32, (ROWS, CAP), 1)
    filled = jnp.int32(0)
    picks = []
    for k in range(BLOCKS):
        source = (shard - k) & (SHARDS - 1)
        block = block_of(routing_ref, source, k)
        count = grids_ref[block, 0, source] * grids_ref[block, 1, source]
        picks.append(jnp.where((row == col + filled) & (col < count), 1.0, 0.0))
        filled = filled + count
    pick = jnp.concatenate(picks, axis=1).astype(BF)
    live = lax.broadcasted_iota(jnp.int32, (ROWS, 512), 0) < filled
    total = jnp.zeros((ROWS, 128), F32)
    for j in range(4):
        column = pl.ds(pl.multiple_of(((y + j) & 3) * 512, 512), 512)
        value = bias_ref[column][None] + sum(p[...].astype(F32) for p in pieces[j])
        image = jnp.dot(pick, value.astype(BF), preferred_element_type=F32)
        value = jnp.where(live, image, text_ref[:, column].astype(F32))
        out_ref[:, column] = value.astype(BF)
        total = total + lane_sums(value)
    sum_ref[...] = row_sums(total)


def norm_kernel(emb_ref, s0, s1, s2, s3, gain_ref, *refs):
    out_ref = refs[-1]
    total = s0[...] + s1[...] + s2[...] + s3[...]
    scale = lax.rsqrt(total / D + EPS).T[:, :1]
    out_ref[...] = (emb_ref[...].astype(F32) * scale * gain_ref[...][None]).astype(BF)


def half(width, which):
    return pl.BlockSpec((ROWS, width), lambda i: (which, 0))


def whole(shape):
    return pl.BlockSpec(shape, lambda i: (0,) * len(shape))


def text_half(text):
    _, width = text.shape
    return pl.pallas_call(
        text_kernel,
        grid=(1,),
        in_specs=[half(width, 1)],
        out_specs=[half(width, 1), whole((8, ROWS))],
        out_shape=[jax.ShapeDtypeStruct(text.shape, BF), jax.ShapeDtypeStruct((8, ROWS), F32)],
        name="text_half",
    )(text)


def splice(idx, routing, grids, pieces, bias, text, emb):
    _, width = text.shape
    return pl.pallas_call(
        splice_kernel,
        grid=(1,),
        in_specs=[SMEM] * 3 + [VMEM] * len(pieces) + [whole((width,)), half(width, 0), ANY],
        out_specs=[half(width, 0), whole((8, ROWS))],
        out_shape=[jax.ShapeDtypeStruct(text.shape, BF), jax.ShapeDtypeStruct((8, ROWS), F32)],
        input_output_aliases={5 + len(pieces): 0},
        name="splice",
    )(idx, routing, grids, *pieces, bias, text, emb)


def norm_half(emb, sums, gain, which, base=None):
    _, width = emb.shape
    args = [emb, *sums, gain]
    specs = [half(width, which)] + [whole((8, ROWS))] * 4 + [whole((width,))]
    alias = {}
    if base is not None:
        args.append(base)
        specs.append(ANY)
        alias = {6: 0}
    return pl.pallas_call(
        norm_kernel,
        grid=(1,),
        in_specs=specs,
        out_specs=half(width, which),
        out_shape=jax.ShapeDtypeStruct(emb.shape, BF),
        input_output_aliases=alias,
    )(*args)


def over_tensor(sums):
    across = shift(sums, xh=1)
    return [sums, shift(sums, c=1), across, shift(across, c=1)]


def per_device(
    patches,
    norm_gain,
    norm_bias,
    first_weight,
    first_bias,
    second_weight,
    second_bias,
    text_embeds,
    final_gain,
    image_grids,
    routing,
):
    idx = lax.axis_index(AXES).astype(jnp.int32).reshape(1)
    routing = routing.T
    grids = jnp.transpose(image_grids, (1, 2, 0))

    weights = {(0, 0): second_weight}
    weights[0, 1] = shift(second_weight, xl=1)
    weights[1, 0] = shift(second_weight, z=1)
    weights[3, 0] = shift(second_weight, z=3)
    weights[1, 1] = shift(weights[0, 1], z=1)
    weights[3, 1] = shift(weights[0, 1], z=3)
    weights[2, 0] = shift(weights[1, 0], z=1)
    weights[2, 1] = shift(weights[3, 1], z=3)
    weights = [weights[chunk] for chunk in CHUNKS]

    blocks = first_product(idx, routing, patches, norm_gain, norm_bias, first_weight, first_bias)
    head = {0: blocks[0]}
    tail = {0: jnp.concatenate([shift_dp(blocks[k], k) for k in range(1, BLOCKS)], axis=0)}
    for j in (1, 3, 2):
        head[j] = shift(head[0], y=j)
        tail[j] = shift(tail[0], y=j)

    def parts(pair):
        return [part[j] for j in pair for part in (head, tail)]

    send_a, rows_a = send_product(idx, parts((1, 3)), weights)
    send_b, rows_b = send_product(idx, parts((2, 0)), weights)
    stay_a, cross_a = keep_product(idx, rows_a, shift(send_a, c=1), weights, False)
    stay_2, stay_0, cross_2, cross_0 = keep_product(idx, rows_b, shift(send_b, c=1), weights, True)
    came_a = shift(cross_a, xh=1)
    came_2 = shift(cross_2, y=2, xh=1)
    came_0 = shift(cross_0, xh=1)
    stay_2 = shift(stay_2, y=2)
    sums_a = [
        (stay_a[at].astype(F32) + came_a[at].astype(F32)).astype(BF) for at in (slice(0, ROWS), slice(ROWS, 2 * ROWS))
    ]
    from_1 = shift(sums_a[0], y=3)
    from_3 = shift(sums_a[1], y=1)

    emb, text_sums = text_half(text_embeds)
    normed = norm_half(emb, over_tensor(text_sums), final_gain, 1)
    pieces = [stay_0, came_0, from_1, stay_2, came_2, from_3]
    emb, sums = splice(idx, routing, grids, pieces, second_bias, text_embeds, emb)
    normed = norm_half(emb, over_tensor(sums), final_gain, 0, normed)
    return (emb, normed)


def solution(mesh):
    mesh = Mesh(mesh.devices.reshape([SIZES[a] for a in AXES]), AXES)
    dp, tensor = ("z", "y", "xl"), ("xh", "c")
    placed = (
        P(dp, None),
        P(),
        P(),
        P(None, tensor),
        P(tensor),
        P(tensor, dp),
        P(tensor),
        P(dp, tensor),
        P(tensor),
        P(),
        P(),
    )
    return jax.shard_map(
        per_device,
        mesh=mesh,
        in_specs=placed,
        out_specs=(P(dp, tensor), P(dp, tensor)),
        check_vma=False,
    )
```

time: 170 us -> 177 us (1.041)
  waiting for transfers between devices: 70.9 us -> 93.4 us
  starting transfers between devices: 48.9 us -> 36.8 us
  Pallas kernels: 36.9 us -> 32.4 us
  local copies, waits for them, and re-layouts: 7.89 us -> 11.3 us
  other arithmetic: 3.66 us -> 1.17 us
    ppermute x28 -> x27, waiting for transfers between devices: 59.2 us -> 82.5 us  [shift(): return lax.ppermute(value, axes, pairs)]
    ppermute x28 -> x27, starting transfers between devices: 44.6 us -> 32.5 us  [shift(): return lax.ppermute(value, axes, pairs)]
    unnamed x41 -> x58, local copies, waits for them, and re-layouts: 6.52 us -> 11.3 us
    pallas_call x4 -> x6, Pallas kernels: 27.9 us -> 24.8 us  [the longest x1 9.04 us: first_product(): pl.pallas_call(first_kernel, in_specs=[SMEM, SMEM] + [ANY] * 5, out_specs...]
    convert_element_type x2 -> x1, other arithmetic: 3.66 us -> 1.17 us  [per_device(): (stay_a[at].astype(F32) + came_a[at].astype(F32)).astype(BF)]
  transfers between devices with their start and end apart: 31 -> 30, of which waited for: 12 -> 13; matrix products, arithmetic and copies ran while one was open for 3% -> 1% of each run, Pallas kernels for 17% -> 14%
where the time goes in v1:
time: 177 us; the launch traced here: 176 us
  waiting for transfers between devices  93.4 us (53%)
  starting transfers between devices  36.8 us (21%)
  Pallas kernels  32.4 us (18%)
  local copies, waits for them, and re-layouts  11.3 us (6%)
    ppermute x27, waiting for transfers between devices, shift(): return lax.ppermute(value, axes, pairs)  82.5 us
    ppermute x27, starting transfers between devices, shift(): return lax.ppermute(value, axes, pairs)  32.5 us
    unnamed x58, local copies, waits for them, and re-layouts  11.3 us
    ppermute x3, waiting for transfers between devices, shift_dp(): return lax.ppermute(value, ('z', 'y', 'xl'), pairs)  10.9 us
    pallas_call x1, Pallas kernels, first_product(): pl.pallas_call(first_kernel, in_specs=[SMEM, SMEM] + [ANY] * 5, out_specs...  9.04 us
    pallas_call x2, Pallas kernels, keep_product(): pl.pallas_call(keep_kernel, in_specs=[SMEM] + [VMEM] * 10, out_specs=[VME...  7.17 us
    pallas_call x2, Pallas kernels, norm_half(): pl.pallas_call(norm_kernel, grid=(1,), in_specs=specs, out_specs=half(wid...  5.33 us
    pallas_call x2, Pallas kernels, send_product(): pl.pallas_call(send_kernel, in_specs=[SMEM] + [VMEM] * 12, out_specs=[VME...  5.08 us
  transfers between devices with their start and end apart: 30, of which 13 were waited for; matrix products, arithmetic and copies ran while one was open for 1% of the time, Pallas kernels for 14%

profile of v1, /device:TPU:1, one launch (start us, length us, event | category | flops | bytes accessed | tf_op | source)
XLA Modules:
  0.0 175.9 jit_solution(13779367569894491764)
XLA Ops:
  0.6 2.1 %collective-permute-start.5 = (bf16[1280,256]{1,0:T(8,128)(2,1)}, bf16[1280,256]{1,0:T(8,128)(2,1)S(1)}, u32[]{:S(2)}, u32[]{:S(2)}) collective-permute-start(bf16[1280,256]{1,0:T(8,128)(2,1)} %refs_0_.3), channel_id=1, source_target_pairs={{0,4},{4,0},{1,5},{5,1},{2,6},{6,2},{3,7},{7,3},{8,12},{12,8},{9,1... | collective-permute-start | bytes 1966088 | tf_op jit(solution)/shard_map/ppermute | solution.py:34
  2.7 1.7 copy-done.7
  4.5 0.7 copy-done.13
  5.2 0.7 copy-done.14
  5.9 0.7 copy-done.15
  6.6 0.7 copy-done.16
  7.3 9.0 %first_product.1 = (bf16[64,1280]{1,0:T(8,128)(2,1)S(1)}, bf16[64,1280]{1,0:T(8,128)(2,1)S(1)}, bf16[64,1280]{1,0:T(8,128)(2,1)S(1)}, bf16[64,1280]{1,0:T(8,128)(2,1)S(1)}) custom-call(s32[1]{0:T(128)} %bitcast.idx_ref, s32[4,32]{1,0:T(4,128)S(1)} %bitcast.4, bf16[1024,1280]{1,0:T(8,128)(2,1)S(1)} %copy-done.7, f32[1280]{0:T(1024)S(1)} %copy-done.13, ...), custom_call_target="tpu_custom_call" | custom-call | tf_op jit(solution)/shard_map/first_product/pallas_call | solution.py:116
  16.3 0.1 collective-permute-start.1
  16.4 1.9 %collective-permute-start.6 = (bf16[1280,256]{1,0:T(8,128)(2,1)S(1)}, bf16[1280,256]{1,0:T(8,128)(2,1)S(1)}, u32[]{:S(2)}, u32[]{:S(2)}) collective-permute-start(bf16[1280,256]{1,0:T(8,128)(2,1)S(1)} %copy-done), channel_id=1, source_target_pairs={{0,32},{32,64},{64,96},{96,0},{1,33},{33,65},{65,97},{97,1},{2,34}... | collective-permute-start | bytes 1966088 | tf_op jit(solution)/shard_map/ppermute | solution.py:34
  18.3 1.3 collective-permute-start.2
  19.6 2.9 %collective-permute-start.3 = (bf16[64,1280]{1,0:T(8,128)(2,1)S(1)}, bf16[64,1280]{1,0:T(8,128)(2,1)S(1)}, u32[]{:S(2)}, u32[]{:S(2)}) collective-permute-start(bf16[64,1280]{1,0:T(8,128)(2,1)S(1)} %get-tuple-element.23), channel_id=1, source_target_pairs={{0,12},{4,16},{8,20},{12,24},{16,28},{20,32},{24,36},{28,40},{32,4... | collective-permute-start | bytes 491528 | tf_op jit(solution)/shard_map/ppermute | solution.py:39
  22.5 4.8 %collective-permute-done.1 = bf16[64,1280]{1,0:T(8,128)(2,1)S(1)} collective-permute-done((bf16[64,1280]{1,0:T(8,128)(2,1)S(1)}, bf16[64,1280]{1,0:T(8,128)(2,1)S(1)}, u32[]{:S(2)}, u32[]{:S(2)}) %collective-permute-start.1) | collective-permute-done | bytes 163872 | tf_op jit(solution)/shard_map/ppermute | solution.py:39
  27.4 0.0 collective-permute-done.5.refs_5_.refs_1_
  27.4 0.7 collective-permute-start.9
  28.1 6.0 %collective-permute-done.2 = bf16[64,1280]{1,0:T(8,128)(2,1)S(1)} collective-permute-done((bf16[64,1280]{1,0:T(8,128)(2,1)S(1)}, bf16[64,1280]{1,0:T(8,128)(2,1)S(1)}, u32[]{:S(2)}, u32[]{:S(2)}) %collective-permute-start.2) | collective-permute-done | bytes 163872 | tf_op jit(solution)/shard_map/ppermute | solution.py:39
  34.2 0.0 collective-permute-done.3
  34.2 0.1 collective-permute-start.15
  34.3 0.1 collective-permute-start.14
  34.4 2.7 %collective-permute-start.16 = (bf16[64,1280]{1,0:T(8,128)(2,1)S(1)}, bf16[64,1280]{1,0:T(8,128)(2,1)S(1)}, u32[]{:S(2)}, u32[]{:S(2)}) collective-permute-start(bf16[64,1280]{1,0:T(8,128)(2,1)S(1)} %get-tuple-element.20.refs_2_), channel_id=1, source_target_pairs={{0,24},{8,0},{16,8},{24,16},{1,25},{9,1},{17,9},{25,17},{2,26},{10... | collective-permute-start | bytes 491528 | tf_op jit(solution)/shard_map/ppermute | solution.py:34
  37.0 13.8 %collective-permute-done.14.refs_0_ = bf16[64,1280]{1,0:T(8,128)(2,1)S(1)} collective-permute-done((bf16[64,1280]{1,0:T(8,128)(2,1)S(1)}, bf16[64,1280]{1,0:T(8,128)(2,1)S(1)}, u32[]{:S(2)}, u32[]{:S(2)}) %collective-permute-start.14) | collective-permute-done | bytes 163872 | tf_op jit(solution)/shard_map/ppermute | solution.py:34
  50.9 1.6 collective-permute-start.11
  52.5 0.0 collective-permute-done.16.refs_2_
  52.5 0.4 collective-permute-start.8
  52.9 2.3 %collective-permute-start.10 = (bf16[1280,256]{1,0:T(8,128)(2,1)S(1)}, bf16[1280,256]{1,0:T(8,128)(2,1)S(1)}, u32[]{:S(2)}, u32[]{:S(2)}) collective-permute-start(bf16[1280,256]{1,0:T(8,128)(2,1)S(1)} %collective-permute-done.9.refs_11_.refs_7_), channel_id=1, source_target_pairs={{0,96},{32,0},{64,32},{96,64},{1,97},{33,1},{65,33},{97,65},{2,98}... | collective-permute-start | bytes 1966088 | tf_op jit(solution)/shard_map/ppermute | solution.py:34
  55.3 10.1 %collective-permute-done.17.refs_3_ = bf16[192,1280]{1,0:T(8,128)(2,1)S(1)} collective-permute-done((bf16[192,1280]{1,0:T(8,128)(2,1)S(1)}, bf16[192,1280]{1,0:T(8,128)(2,1)S(1)}, u32[]{:S(2)}, u32[]{:S(2)}) %collective-permute-start.17) | collective-permute-done | bytes 491552 | tf_op jit(solution)/shard_map/ppermute | solution.py:34
  65.4 2.6 %collective-permute-done.7.refs_7_.refs_3_ = bf16[1280,256]{1,0:T(8,128)(2,1)S(1)} collective-permute-done((bf16[1280,256]{1,0:T(8,128)(2,1)S(1)}, bf16[1280,256]{1,0:T(8,128)(2,1)S(1)}, u32[]{:S(2)}, u32[]{:S(2)}) %collective-permute-start.7) | collective-permute-done | bytes 655392 | tf_op jit(solution)/shard_map/ppermute | solution.py:34
  68.0 14.0 %collective-permute-done.8.refs_8_.refs_4_ = bf16[1280,256]{1,0:T(8,128)(2,1)S(1)} collective-permute-done((bf16[1280,256]{1,0:T(8,128)(2,1)S(1)}, bf16[1280,256]{1,0:T(8,128)(2,1)S(1)}, u32[]{:S(2)}, u32[]{:S(2)}) %collective-permute-start.8) | collective-permute-done | bytes 655392 | tf_op jit(solution)/shard_map/ppermute | solution.py:34
  82.1 2.1 %shard_map.124 = (bf16[2,512,512]{2,1,0:T(8,128)(2,1)S(1)}, bf16[512,1280]{1,0:T(8,128)(2,1)S(1)}) custom-call(s32[1]{0:T(128)} %bitcast.idx_ref, bf16[64,1280]{1,0:T(8,128)(2,1)S(1)} %collective-permute-done.14.refs_0_, bf16[192,1280]{1,0:T(8,128)(2,1)S(1)} %collective-permute-done.15.refs_1_, bf16[64,1280]{1,0:T(8,128)(2,1)S(1)} %collective-permute-done.16.refs_2_, ...), custom_call_target="tpu_custom_call" | custom-call | tf_op jit(solution)/shard_map/pallas_call | solution.py:194
  84.2 2.8 %collective-permute-start.18 = (bf16[2,512,512]{2,1,0:T(8,128)(2,1)S(1)}, bf16[2,512,512]{2,1,0:T(8,128)(2,1)S(1)}, u32[]{:S(2)}, u32[]{:S(2)}) collective-permute-start(bf16[2,512,512]{2,1,0:T(8,128)(2,1)S(1)} %get-tuple-element.29), channel_id=1, source_target_pairs={{0,1},{1,0},{2,3},{3,2},{4,5},{5,4},{6,7},{7,6},{8,9},{9,8},{10,11... | collective-permute-start | bytes 3145736 | tf_op jit(solution)/shard_map/ppermute | solution.py:34
  87.0 3.0 %collective-permute-start = (bf16[64,1280]{1,0:T(8,128)(2,1)S(1)}, bf16[64,1280]{1,0:T(8,128)(2,1)S(1)}, u32[]{:S(2)}, u32[]{:S(2)}) collective-permute-start(bf16[64,1280]{1,0:T(8,128)(2,1)S(1)} %get-tuple-element.20.refs_2_), channel_id=1, source_target_pairs={{0,16},{8,24},{16,0},{24,8},{1,17},{9,25},{17,1},{25,9},{2,18},{10... | collective-permute-start | bytes 491528 | tf_op jit(solution)/shard_map/ppermute | solution.py:34
  89.9 14.7 %collective-permute-done.refs_0_ = bf16[64,1280]{1,0:T(8,128)(2,1)S(1)} collective-permute-done((bf16[64,1280]{1,0:T(8,128)(2,1)S(1)}, bf16[64,1280]{1,0:T(8,128)(2,1)S(1)}, u32[]{:S(2)}, u32[]{:S(2)}) %collective-permute-start) | collective-permute-done | bytes 163872 | tf_op jit(solution)/shard_map/ppermute | solution.py:34
  104.7 2.9 %shard_map.122 = (bf16[2,512,512]{2,1,0:T(8,128)(2,1)}, bf16[512,1280]{1,0:T(8,128)(2,1)S(1)}) custom-call(s32[1]{0:T(128)} %bitcast.idx_ref, bf16[64,1280]{1,0:T(8,128)(2,1)S(1)} %collective-permute-done.refs_0_, bf16[192,1280]{1,0:T(8,128)(2,1)S(1)} %collective-permute-done.4.refs_1_, bf16[64,1280]{1,0:T(8,128)(2,1)S(1)} %get-tuple-element.20.refs_2_, ...), custom_call_target="tpu_custom_call" | custom-call | tf_op jit(solution)/shard_map/pallas_call | solution.py:194
  107.6 0.8 collective-permute-start.12
  108.4 3.0 %shard_map.125 = (bf16[512,512]{1,0:T(8,128)(2,1)S(1)}, bf16[512,512]{1,0:T(8,128)(2,1)}) custom-call(s32[1]{0:T(128)} %bitcast.idx_ref, bf16[512,1280]{1,0:T(8,128)(2,1)S(1)} %get-tuple-element.28.rows, bf16[2,512,512]{2,1,0:T(8,128)(2,1)S(1)} %collective-permute-done.18.came, bf16[1280,256]{1,0:T(8,128)(2,1)S(1)} %copy-done, ...), custom_call_target="tpu_custom_call" | custom-call | tf_op jit(solution)/shard_map/pallas_call | solution.py:205
  111.4 0.8 copy-done.10
  112.2 3.3 %collective-permute-start.19 = (bf16[512,512]{1,0:T(8,128)(2,1)}, bf16[512,512]{1,0:T(8,128)(2,1)}, u32[]{:S(2)}, u32[]{:S(2)}) collective-permute-start(bf16[512,512]{1,0:T(8,128)(2,1)} %get-tuple-element.31), channel_id=1, source_target_pairs={{0,2},{2,0},{1,3},{3,1},{4,6},{6,4},{5,7},{7,5},{8,10},{10,8},{9,1... | collective-permute-start | bytes 1572872 | tf_op jit(solution)/shard_map/ppermute | solution.py:34
  115.5 2.4 %text_half.1 = (bf16[512,2048]{1,0:T(8,128)(2,1)}, f32[8,256]{1,0:T(8,128)}) custom-call(bf16[512,2048]{1,0:T(8,128)(2,1)} %refs_7_.1), custom_call_target="tpu_custom_call" | custom-call | tf_op jit(solution)/shard_map/text_half/pallas_call | solution.py:274
  117.9 0.0 collective-permute-start.28
  117.9 0.3 collective-permute-start.27
  118.2 10.1 %collective-permute-done.28.s2 = f32[8,256]{1,0:T(8,128)S(1)} collective-permute-done((f32[8,256]{1,0:T(8,128)}, f32[8,256]{1,0:T(8,128)S(1)}, u32[]{:S(2)}, u32[]{:S(2)}) %collective-permute-start.28) | collective-permute-done | bytes 8224 | tf_op jit(solution)/shard_map/ppermute | solution.py:34
  128.3 0.5 collective-permute-start.29
  128.8 1.1 copy-done.2
  129.9 1.1 copy-done.4
  131.0 1.1 copy-done.6
  132.1 1.3 copy-done.9
  133.4 4.2 %shard_map.123 = (bf16[256,512]{1,0:T(8,128)(2,1)}, bf16[256,512]{1,0:T(8,128)(2,1)S(1)}, bf16[256,512]{1,0:T(8,128)(2,1)S(1)}, bf16[256,512]{1,0:T(8,128)(2,1)}) custom-call(s32[1]{0:T(128)} %bitcast.idx_ref, bf16[512,1280]{1,0:T(8,128)(2,1)S(1)} %copy-done.9, bf16[2,512,512]{2,1,0:T(8,128)(2,1)} %collective-permute-done.12.came, ...), custom_call_target="tpu_custom_call" | custom-call | tf_op jit(solution)/shard_map/pallas_call | solution.py:205
  137.6 3.0 %collective-permute-start.13 = (bf16[256,512]{1,0:T(8,128)(2,1)}, bf16[256,512]{1,0:T(8,128)(2,1)S(1)}, u32[]{:S(2)}, u32[]{:S(2)}) collective-permute-start(bf16[256,512]{1,0:T(8,128)(2,1)} %get-tuple-element.27), channel_id=1, source_target_pairs={{0,2},{2,0},{1,3},{3,1},{4,6},{6,4},{5,7},{7,5},{8,10},{10,8},{9,1... | collective-permute-start | bytes 786440 | tf_op jit(solution)/shard_map/ppermute | solution.py:34
  140.6 2.8 %collective-permute-start.22 = (bf16[256,512]{1,0:T(8,128)(2,1)S(1)}, bf16[256,512]{1,0:T(8,128)(2,1)S(1)}, u32[]{:S(2)}, u32[]{:S(2)}) collective-permute-start(bf16[256,512]{1,0:T(8,128)(2,1)S(1)} %get-tuple-element.33), channel_id=1, source_target_pairs={{0,18},{2,16},{8,26},{10,24},{16,2},{18,0},{24,10},{26,8},{1,19},{... | collective-permute-start | bytes 786440 | tf_op jit(solution)/shard_map/ppermute | solution.py:34
  143.4 1.2 add_convert_fusion
  144.6 0.1 collective-permute-start.20
  144.7 1.4 collective-permute-start.23
  146.1 2.7 %shard_map.126.refs_0_ = bf16[512,2048]{1,0:T(8,128)(2,1)} custom-call(bf16[512,2048]{1,0:T(8,128)(2,1)} %get-tuple-element.34.refs_8_.emb_ref, f32[8,256]{1,0:T(8,128)} %get-tuple-element.37.s0, f32[8,256]{1,0:T(8,128)} %copy-done.23, f32[8,256]{1,0:T(8,128)} %copy-done.22, f32[8,256]{1,0:T(8,128)} %copy-done.24, f32[2048]{0:T(1024)} %gain_ref.3), custom_call_target="tpu_custom_call" | custom-call | tf_op jit(solution)/shard_map/pallas_call | solution.py:306
  148.8 6.8 %collective-permute-done.21.refs_3_ = bf16[256,512]{1,0:T(8,128)(2,1)S(1)} collective-permute-done((bf16[256,512]{1,0:T(8,128)(2,1)}, bf16[256,512]{1,0:T(8,128)(2,1)S(1)}, u32[]{:S(2)}, u32[]{:S(2)}) %collective-permute-start.21) | collective-permute-done | bytes 262176 | tf_op jit(solution)/shard_map/ppermute | solution.py:34
  155.6 2.5 %collective-permute-done.20.refs_2_ = bf16[256,512]{1,0:T(8,128)(2,1)S(1)} collective-permute-done((bf16[256,512]{1,0:T(8,128)(2,1)S(1)}, bf16[256,512]{1,0:T(8,128)(2,1)S(1)}, u32[]{:S(2)}, u32[]{:S(2)}) %collective-permute-start.20) | collective-permute-done | bytes 262176 | tf_op jit(solution)/shard_map/ppermute | solution.py:34
  158.0 3.7 %collective-permute-done.23.refs_5_ = bf16[256,512]{1,0:T(8,128)(2,1)S(1)} collective-permute-done((bf16[256,512]{1,0:T(8,128)(2,1)S(1)}, bf16[256,512]{1,0:T(8,128)(2,1)S(1)}, u32[]{:S(2)}, u32[]{:S(2)}) %collective-permute-start.23) | collective-permute-done | bytes 262176 | tf_op jit(solution)/shard_map/ppermute | solution.py:34
  161.8 0.7 copy-done.21
  162.5 3.5 %splice.1 = (bf16[512,2048]{1,0:T(8,128)(2,1)}, f32[8,256]{1,0:T(8,128)}) custom-call(s32[1]{0:T(128)} %bitcast.idx_ref, s32[4,32]{1,0:T(4,128)} %bitcast.3, s32[4,2,32]{2,1,0:T(2,128)} %bitcast.5, bf16[256,512]{1,0:T(8,128)(2,1)} %copy-done.12, bf16[256,512]{1,0:T(8,128)(2,1)} %copy-done.17, ...), custom_call_target="tpu_custom_call", output_to_operand_aliasing={{0}: (11, {})} | custom-call | tf_op jit(solution)/shard_map/splice/pallas_call | solution.py:286
  165.9 0.3 collective-permute-start.25
  166.2 0.8 collective-permute-start.24
  167.0 3.2 %collective-permute-done.25.s2 = f32[8,256]{1,0:T(8,128)S(1)} collective-permute-done((f32[8,256]{1,0:T(8,128)}, f32[8,256]{1,0:T(8,128)S(1)}, u32[]{:S(2)}, u32[]{:S(2)}) %collective-permute-start.25) | collective-permute-done | bytes 8224 | tf_op jit(solution)/shard_map/ppermute | solution.py:34
  170.2 1.6 collective-permute-start.26
  171.8 0.8 collective-permute-done.26.s3
  172.6 0.6 copy-done.27
  173.2 2.7 %shard_map.127 = bf16[512,2048]{1,0:T(8,128)(2,1)} custom-call(bf16[512,2048]{1,0:T(8,128)(2,1)} %get-tuple-element.18.emb_ref, f32[8,256]{1,0:T(8,128)} %get-tuple-element.36.s0, f32[8,256]{1,0:T(8,128)} %copy-done.26, f32[8,256]{1,0:T(8,128)} %copy-done.25, f32[8,256]{1,0:T(8,128)} %copy-done.27, f32[2048]{0:T(1024)} %gain_ref.3, ...), custom_call_target="tpu_custom_call", output_to_operand_aliasing={{}: (6, {})} | custom-call | tf_op jit(solution)/shard_map/pallas_call | solution.py:306
  (65 shorter events, 0.2 us)
Async XLA Ops:
  0.6 26.7 %collective-permute-start.5 = (bf16[1280,256]{1,0:T(8,128)(2,1)}, bf16[1280,256]{1,0:T(8,128)(2,1)S(1)}, u32[]{:S(2)}, u32[]{:S(2)}) collective-permute-start(bf16[1280,256]{1,0:T(8,128)(2,1)} %refs_0_.3), channel_id=1, source_target_pairs={{0,4},{4,0},{1,5},{5,1},{2,6},{6,2},{3,7},{7,3},{8,12},{12,8},{9,1... | collective-permute-start | bytes 1966088 | tf_op jit(solution)/shard_map/ppermute | solution.py:34
  2.7 1.7 copy-start.7
  4.5 0.7 copy-start.13
  5.2 0.7 copy-start.14
  5.9 0.7 copy-start.15
  6.6 0.7 copy-start.16
  7.3 9.1 %copy-start = (bf16[1280,256]{1,0:T(8,128)(2,1)S(1)}, bf16[1280,256]{1,0:T(8,128)(2,1)}, u32[]{:S(2)}) copy-start(bf16[1280,256]{1,0:T(8,128)(2,1)} %refs_0_.3) | copy-start | bytes 1966084
  16.3 11.0 %collective-permute-start.1 = (bf16[64,1280]{1,0:T(8,128)(2,1)S(1)}, bf16[64,1280]{1,0:T(8,128)(2,1)S(1)}, u32[]{:S(2)}, u32[]{:S(2)}) collective-permute-start(bf16[64,1280]{1,0:T(8,128)(2,1)S(1)} %get-tuple-element.21), channel_id=1, source_target_pairs={{0,4},{4,8},{8,12},{12,16},{16,20},{20,24},{24,28},{28,32},{32,36}... | collective-permute-start | bytes 491528 | tf_op jit(solution)/shard_map/ppermute | solution.py:39
  16.4 36.1 %collective-permute-start.6 = (bf16[1280,256]{1,0:T(8,128)(2,1)S(1)}, bf16[1280,256]{1,0:T(8,128)(2,1)S(1)}, u32[]{:S(2)}, u32[]{:S(2)}) collective-permute-start(bf16[1280,256]{1,0:T(8,128)(2,1)S(1)} %copy-done), channel_id=1, source_target_pairs={{0,32},{32,64},{64,96},{96,0},{1,33},{33,65},{65,97},{97,1},{2,34}... | collective-permute-start | bytes 1966088 | tf_op jit(solution)/shard_map/ppermute | solution.py:34
  18.3 15.9 %collective-permute-start.2 = (bf16[64,1280]{1,0:T(8,128)(2,1)S(1)}, bf16[64,1280]{1,0:T(8,128)(2,1)S(1)}, u32[]{:S(2)}, u32[]{:S(2)}) collective-permute-start(bf16[64,1280]{1,0:T(8,128)(2,1)S(1)} %get-tuple-element.22), channel_id=1, source_target_pairs={{0,8},{4,12},{8,16},{12,20},{16,24},{20,28},{24,32},{28,36},{32,40... | collective-permute-start | bytes 491528 | tf_op jit(solution)/shard_map/ppermute | solution.py:39
  19.6 14.6 %collective-permute-start.3 = (bf16[64,1280]{1,0:T(8,128)(2,1)S(1)}, bf16[64,1280]{1,0:T(8,128)(2,1)S(1)}, u32[]{:S(2)}, u32[]{:S(2)}) collective-permute-start(bf16[64,1280]{1,0:T(8,128)(2,1)S(1)} %get-tuple-element.23), channel_id=1, source_target_pairs={{0,12},{4,16},{8,20},{12,24},{16,28},{20,32},{24,36},{28,40},{32,4... | collective-permute-start | bytes 491528 | tf_op jit(solution)/shard_map/ppermute | solution.py:39
  27.4 25.5 %collective-permute-start.9 = (bf16[1280,256]{1,0:T(8,128)(2,1)S(1)}, bf16[1280,256]{1,0:T(8,128)(2,1)S(1)}, u32[]{:S(2)}, u32[]{:S(2)}) collective-permute-start(bf16[1280,256]{1,0:T(8,128)(2,1)S(1)} %collective-permute-done.5.refs_5_.refs_1_), channel_id=1, source_target_pairs={{0,96},{32,0},{64,32},{96,64},{1,97},{33,1},{65,33},{97,65},{2,98}... | collective-permute-start | bytes 1966088 | tf_op jit(solution)/shard_map/ppermute | solution.py:34
  34.2 21.1 %collective-permute-start.15 = (bf16[192,1280]{1,0:T(8,128)(2,1)S(1)}, bf16[192,1280]{1,0:T(8,128)(2,1)S(1)}, u32[]{:S(2)}, u32[]{:S(2)}) collective-permute-start(bf16[192,1280]{1,0:T(8,128)(2,1)S(1)} %constant_dynamic-update-slice_fusion.refs_3_), channel_id=1, source_target_pairs={{0,8},{8,16},{16,24},{24,0},{1,9},{9,17},{17,25},{25,1},{2,10},{10... | collective-permute-start | bytes 1474568 | tf_op jit(solution)/shard_map/ppermute | solution.py:34
  34.3 16.6 %collective-permute-start.14 = (bf16[64,1280]{1,0:T(8,128)(2,1)S(1)}, bf16[64,1280]{1,0:T(8,128)(2,1)S(1)}, u32[]{:S(2)}, u32[]{:S(2)}) collective-permute-start(bf16[64,1280]{1,0:T(8,128)(2,1)S(1)} %get-tuple-element.20.refs_2_), channel_id=1, source_target_pairs={{0,8},{8,16},{16,24},{24,0},{1,9},{9,17},{17,25},{25,1},{2,10},{10... | collective-permute-start | bytes 491528 | tf_op jit(solution)/shard_map/ppermute | solution.py:34
  34.4 18.1 %collective-permute-start.16 = (bf16[64,1280]{1,0:T(8,128)(2,1)S(1)}, bf16[64,1280]{1,0:T(8,128)(2,1)S(1)}, u32[]{:S(2)}, u32[]{:S(2)}) collective-permute-start(bf16[64,1280]{1,0:T(8,128)(2,1)S(1)} %get-tuple-element.20.refs_2_), channel_id=1, source_target_pairs={{0,24},{8,0},{16,8},{24,16},{1,25},{9,1},{17,9},{25,17},{2,26},{10... | collective-permute-start | bytes 491528 | tf_op jit(solution)/shard_map/ppermute | solution.py:34
  50.9 14.5 %collective-permute-start.11 = (bf16[1280,256]{1,0:T(8,128)(2,1)S(1)}, bf16[1280,256]{1,0:T(8,128)(2,1)S(1)}, u32[]{:S(2)}, u32[]{:S(2)}) collective-permute-start(bf16[1280,256]{1,0:T(8,128)(2,1)S(1)} %copy-done), channel_id=1, source_target_pairs={{0,96},{32,0},{64,32},{96,64},{1,97},{33,1},{65,33},{97,65},{2,98}... | collective-permute-start | bytes 1966088 | tf_op jit(solution)/shard_map/ppermute | solution.py:34
  52.5 15.5 %collective-permute-start.7 = (bf16[1280,256]{1,0:T(8,128)(2,1)S(1)}, bf16[1280,256]{1,0:T(8,128)(2,1)S(1)}, u32[]{:S(2)}, u32[]{:S(2)}) collective-permute-start(bf16[1280,256]{1,0:T(8,128)(2,1)S(1)} %collective-permute-done.5.refs_5_.refs_1_), channel_id=1, source_target_pairs={{0,32},{32,64},{64,96},{96,0},{1,33},{33,65},{65,97},{97,1},{2,34}... | collective-permute-start | bytes 1966088 | tf_op jit(solution)/shard_map/ppermute | solution.py:34
  52.5 29.6 %collective-permute-start.8 = (bf16[1280,256]{1,0:T(8,128)(2,1)S(1)}, bf16[1280,256]{1,0:T(8,128)(2,1)S(1)}, u32[]{:S(2)}, u32[]{:S(2)}) collective-permute-start(bf16[1280,256]{1,0:T(8,128)(2,1)S(1)} %collective-permute-done.6.refs_6_.refs_2_), channel_id=1, source_target_pairs={{0,32},{32,64},{64,96},{96,0},{1,33},{33,65},{65,97},{97,1},{2,34}... | collective-permute-start | bytes 1966088 | tf_op jit(solution)/shard_map/ppermute | solution.py:34
  52.9 29.1 %collective-permute-start.10 = (bf16[1280,256]{1,0:T(8,128)(2,1)S(1)}, bf16[1280,256]{1,0:T(8,128)(2,1)S(1)}, u32[]{:S(2)}, u32[]{:S(2)}) collective-permute-start(bf16[1280,256]{1,0:T(8,128)(2,1)S(1)} %collective-permute-done.9.refs_11_.refs_7_), channel_id=1, source_target_pairs={{0,96},{32,0},{64,32},{96,64},{1,97},{33,1},{65,33},{97,65},{2,98}... | collective-permute-start | bytes 1966088 | tf_op jit(solution)/shard_map/ppermute | solution.py:34
  55.3 10.1 %collective-permute-start.17 = (bf16[192,1280]{1,0:T(8,128)(2,1)S(1)}, bf16[192,1280]{1,0:T(8,128)(2,1)S(1)}, u32[]{:S(2)}, u32[]{:S(2)}) collective-permute-start(bf16[192,1280]{1,0:T(8,128)(2,1)S(1)} %constant_dynamic-update-slice_fusion.refs_3_), channel_id=1, source_target_pairs={{0,24},{8,0},{16,8},{24,16},{1,25},{9,1},{17,9},{25,17},{2,26},{10... | collective-permute-start | bytes 1474568 | tf_op jit(solution)/shard_map/ppermute | solution.py:34
  68.0 40.4 %copy-start.1 = (bf16[1280,256]{1,0:T(8,128)(2,1)}, bf16[1280,256]{1,0:T(8,128)(2,1)S(1)}, u32[]{:S(2)}) copy-start(bf16[1280,256]{1,0:T(8,128)(2,1)S(1)} %collective-permute-done.7.refs_7_.refs_3_) | copy-start | bytes 1966084
  82.1 26.4 %copy-start.3 = (bf16[1280,256]{1,0:T(8,128)(2,1)}, bf16[1280,256]{1,0:T(8,128)(2,1)S(1)}, u32[]{:S(2)}) copy-start(bf16[1280,256]{1,0:T(8,128)(2,1)S(1)} %collective-permute-done.8.refs_8_.refs_4_) | copy-start | bytes 1966084
  82.1 26.4 %copy-start.5 = (bf16[1280,256]{1,0:T(8,128)(2,1)}, bf16[1280,256]{1,0:T(8,128)(2,1)S(1)}, u32[]{:S(2)}) copy-start(bf16[1280,256]{1,0:T(8,128)(2,1)S(1)} %collective-permute-done.10.refs_9_.refs_5_) | copy-start | bytes 1966084
  84.2 24.2 %collective-permute-start.18 = (bf16[2,512,512]{2,1,0:T(8,128)(2,1)S(1)}, bf16[2,512,512]{2,1,0:T(8,128)(2,1)S(1)}, u32[]{:S(2)}, u32[]{:S(2)}) collective-permute-start(bf16[2,512,512]{2,1,0:T(8,128)(2,1)S(1)} %get-tuple-element.29), channel_id=1, source_target_pairs={{0,1},{1,0},{2,3},{3,2},{4,5},{5,4},{6,7},{7,6},{8,9},{9,8},{10,11... | collective-permute-start | bytes 3145736 | tf_op jit(solution)/shard_map/ppermute | solution.py:34
  87.0 17.7 %collective-permute-start.4 = (bf16[192,1280]{1,0:T(8,128)(2,1)S(1)}, bf16[192,1280]{1,0:T(8,128)(2,1)S(1)}, u32[]{:S(2)}, u32[]{:S(2)}) collective-permute-start(bf16[192,1280]{1,0:T(8,128)(2,1)S(1)} %constant_dynamic-update-slice_fusion.refs_3_), channel_id=1, source_target_pairs={{0,16},{8,24},{16,0},{24,8},{1,17},{9,25},{17,1},{25,9},{2,18},{10... | collective-permute-start | bytes 1474568 | tf_op jit(solution)/shard_map/ppermute | solution.py:34
  87.0 17.7 %collective-permute-start = (bf16[64,1280]{1,0:T(8,128)(2,1)S(1)}, bf16[64,1280]{1,0:T(8,128)(2,1)S(1)}, u32[]{:S(2)}, u32[]{:S(2)}) collective-permute-start(bf16[64,1280]{1,0:T(8,128)(2,1)S(1)} %get-tuple-element.20.refs_2_), channel_id=1, source_target_pairs={{0,16},{8,24},{16,0},{24,8},{1,17},{9,25},{17,1},{25,9},{2,18},{10... | collective-permute-start | bytes 491528 | tf_op jit(solution)/shard_map/ppermute | solution.py:34
  107.6 3.8 %copy-start.8 = (bf16[512,1280]{1,0:T(8,128)(2,1)}, bf16[512,1280]{1,0:T(8,128)(2,1)S(1)}, u32[]{:S(2)}) copy-start(bf16[512,1280]{1,0:T(8,128)(2,1)S(1)} %get-tuple-element.24.rows) | copy-start | bytes 3932164
  107.6 21.2 %collective-permute-start.12 = (bf16[2,512,512]{2,1,0:T(8,128)(2,1)}, bf16[2,512,512]{2,1,0:T(8,128)(2,1)}, u32[]{:S(2)}, u32[]{:S(2)}) collective-permute-start(bf16[2,512,512]{2,1,0:T(8,128)(2,1)} %get-tuple-element.25), channel_id=1, source_target_pairs={{0,1},{1,0},{2,3},{3,2},{4,5},{5,4},{6,7},{7,6},{8,9},{9,8},{10,11... | collective-permute-start | bytes 3145736 | tf_op jit(solution)/shard_map/ppermute | solution.py:34
  111.4 0.8 copy-start.10
  112.2 28.4 %collective-permute-start.19 = (bf16[512,512]{1,0:T(8,128)(2,1)}, bf16[512,512]{1,0:T(8,128)(2,1)}, u32[]{:S(2)}, u32[]{:S(2)}) collective-permute-start(bf16[512,512]{1,0:T(8,128)(2,1)} %get-tuple-element.31), channel_id=1, source_target_pairs={{0,2},{2,0},{1,3},{3,1},{4,6},{6,4},{5,7},{7,5},{8,10},{10,8},{9,1... | collective-permute-start | bytes 1572872 | tf_op jit(solution)/shard_map/ppermute | solution.py:34
  117.9 10.4 %collective-permute-start.28 = (f32[8,256]{1,0:T(8,128)}, f32[8,256]{1,0:T(8,128)S(1)}, u32[]{:S(2)}, u32[]{:S(2)}) collective-permute-start(f32[8,256]{1,0:T(8,128)} %get-tuple-element.37.s0), channel_id=1, source_target_pairs={{0,2},{2,0},{1,3},{3,1},{4,6},{6,4},{5,7},{7,5},{8,10},{10,8},{9,1... | collective-permute-start | bytes 24584 | tf_op jit(solution)/shard_map/ppermute | solution.py:34
  117.9 26.7 %collective-permute-start.27 = (f32[8,256]{1,0:T(8,128)}, f32[8,256]{1,0:T(8,128)S(1)}, u32[]{:S(2)}, u32[]{:S(2)}) collective-permute-start(f32[8,256]{1,0:T(8,128)} %get-tuple-element.37.s0), channel_id=1, source_target_pairs={{0,1},{1,0},{2,3},{3,2},{4,5},{5,4},{6,7},{7,6},{8,9},{9,8},{10,11... | collective-permute-start | bytes 24584 | tf_op jit(solution)/shard_map/ppermute | solution.py:34
  128.3 9.3 %copy-start.22 = (f32[8,256]{1,0:T(8,128)}, f32[8,256]{1,0:T(8,128)S(1)}, u32[]{:S(2)}) copy-start(f32[8,256]{1,0:T(8,128)S(1)} %collective-permute-done.28.s2) | copy-start | bytes 24580
  128.3 16.3 %collective-permute-start.29 = (f32[8,256]{1,0:T(8,128)S(1)}, f32[8,256]{1,0:T(8,128)S(1)}, u32[]{:S(2)}, u32[]{:S(2)}) collective-permute-start(f32[8,256]{1,0:T(8,128)S(1)} %collective-permute-done.28.s2), channel_id=1, source_target_pairs={{0,1},{1,0},{2,3},{3,2},{4,5},{5,4},{6,7},{7,6},{8,9},{9,8},{10,11... | collective-permute-start | bytes 24584 | tf_op jit(solution)/shard_map/ppermute | solution.py:34
  128.8 1.1 copy-start.2
  129.9 1.1 copy-start.4
  131.0 1.1 copy-start.6
  132.1 1.3 copy-start.9
  133.4 10.0 %copy-start.11 = (bf16[512,512]{1,0:T(8,128)(2,1)S(1)}, bf16[512,512]{1,0:T(8,128)(2,1)}, u32[]{:S(2)}) copy-start(bf16[512,512]{1,0:T(8,128)(2,1)} %copy-done.10) | copy-start | bytes 1572868
  137.6 6.9 %copy-start.12 = (bf16[256,512]{1,0:T(8,128)(2,1)}, bf16[256,512]{1,0:T(8,128)(2,1)S(1)}, u32[]{:S(2)}) copy-start(bf16[256,512]{1,0:T(8,128)(2,1)S(1)} %get-tuple-element.26.refs_0_) | copy-start | bytes 786436
  137.6 11.2 %collective-permute-start.13 = (bf16[256,512]{1,0:T(8,128)(2,1)}, bf16[256,512]{1,0:T(8,128)(2,1)S(1)}, u32[]{:S(2)}, u32[]{:S(2)}) collective-permute-start(bf16[256,512]{1,0:T(8,128)(2,1)} %get-tuple-element.27), channel_id=1, source_target_pairs={{0,2},{2,0},{1,3},{3,1},{4,6},{6,4},{5,7},{7,5},{8,10},{10,8},{9,1... | collective-permute-start | bytes 786440 | tf_op jit(solution)/shard_map/ppermute | solution.py:34
  140.6 15.0 %collective-permute-start.21 = (bf16[256,512]{1,0:T(8,128)(2,1)}, bf16[256,512]{1,0:T(8,128)(2,1)S(1)}, u32[]{:S(2)}, u32[]{:S(2)}) collective-permute-start(bf16[256,512]{1,0:T(8,128)(2,1)} %get-tuple-element.32), channel_id=1, source_target_pairs={{0,16},{8,24},{16,0},{24,8},{1,17},{9,25},{17,1},{25,9},{2,18},{10... | collective-permute-start | bytes 786440 | tf_op jit(solution)/shard_map/ppermute | solution.py:34
  140.6 15.0 %collective-permute-start.22 = (bf16[256,512]{1,0:T(8,128)(2,1)S(1)}, bf16[256,512]{1,0:T(8,128)(2,1)S(1)}, u32[]{:S(2)}, u32[]{:S(2)}) collective-permute-start(bf16[256,512]{1,0:T(8,128)(2,1)S(1)} %get-tuple-element.33), channel_id=1, source_target_pairs={{0,18},{2,16},{8,26},{10,24},{16,2},{18,0},{24,10},{26,8},{1,19},{... | collective-permute-start | bytes 786440 | tf_op jit(solution)/shard_map/ppermute | solution.py:34
  144.6 1.6 copy-start.23
  144.6 13.5 %collective-permute-start.20 = (bf16[256,512]{1,0:T(8,128)(2,1)S(1)}, bf16[256,512]{1,0:T(8,128)(2,1)S(1)}, u32[]{:S(2)}, u32[]{:S(2)}) collective-permute-start(bf16[256,512]{1,0:T(8,128)(2,1)S(1)} %get-tuple-element.39), channel_id=1, source_target_pairs={{0,24},{8,0},{16,8},{24,16},{1,25},{9,1},{17,9},{25,17},{2,26},{10... | collective-permute-start | bytes 786440 | tf_op jit(solution)/shard_map/ppermute | solution.py:34
  144.7 1.5 copy-start.24
  144.7 17.1 %collective-permute-start.23 = (bf16[256,512]{1,0:T(8,128)(2,1)S(1)}, bf16[256,512]{1,0:T(8,128)(2,1)S(1)}, u32[]{:S(2)}, u32[]{:S(2)}) collective-permute-start(bf16[256,512]{1,0:T(8,128)(2,1)S(1)} %get-tuple-element.38), channel_id=1, source_target_pairs={{0,8},{8,16},{16,24},{24,0},{1,9},{9,17},{17,25},{25,1},{2,10},{10... | collective-permute-start | bytes 786440 | tf_op jit(solution)/shard_map/ppermute | solution.py:34
  148.8 13.0 %copy-start.17 = (bf16[256,512]{1,0:T(8,128)(2,1)}, bf16[256,512]{1,0:T(8,128)(2,1)S(1)}, u32[]{:S(2)}) copy-start(bf16[256,512]{1,0:T(8,128)(2,1)S(1)} %collective-permute-done.13.refs_1_) | copy-start | bytes 786436
  155.6 6.2 %copy-start.18 = (bf16[256,512]{1,0:T(8,128)(2,1)}, bf16[256,512]{1,0:T(8,128)(2,1)S(1)}, u32[]{:S(2)}) copy-start(bf16[256,512]{1,0:T(8,128)(2,1)S(1)} %collective-permute-done.21.refs_3_) | copy-start | bytes 786436
  155.6 6.2 %copy-start.19 = (bf16[256,512]{1,0:T(8,128)(2,1)}, bf16[256,512]{1,0:T(8,128)(2,1)S(1)}, u32[]{:S(2)}) copy-start(bf16[256,512]{1,0:T(8,128)(2,1)S(1)} %collective-permute-done.22.refs_4_) | copy-start | bytes 786436
  158.0 3.7 %copy-start.20 = (bf16[256,512]{1,0:T(8,128)(2,1)}, bf16[256,512]{1,0:T(8,128)(2,1)S(1)}, u32[]{:S(2)}) copy-start(bf16[256,512]{1,0:T(8,128)(2,1)S(1)} %collective-permute-done.20.refs_2_) | copy-start | bytes 786436
  161.8 0.7 copy-start.21
  165.9 4.2 %collective-permute-start.25 = (f32[8,256]{1,0:T(8,128)}, f32[8,256]{1,0:T(8,128)S(1)}, u32[]{:S(2)}, u32[]{:S(2)}) collective-permute-start(f32[8,256]{1,0:T(8,128)} %get-tuple-element.36.s0), channel_id=1, source_target_pairs={{0,2},{2,0},{1,3},{3,1},{4,6},{6,4},{5,7},{7,5},{8,10},{10,8},{9,1... | collective-permute-start | bytes 24584 | tf_op jit(solution)/shard_map/ppermute | solution.py:34
  166.2 5.6 %collective-permute-start.24 = (f32[8,256]{1,0:T(8,128)}, f32[8,256]{1,0:T(8,128)S(1)}, u32[]{:S(2)}, u32[]{:S(2)}) collective-permute-start(f32[8,256]{1,0:T(8,128)} %get-tuple-element.36.s0), channel_id=1, source_target_pairs={{0,1},{1,0},{2,3},{3,2},{4,5},{5,4},{6,7},{7,6},{8,9},{9,8},{10,11... | collective-permute-start | bytes 24584 | tf_op jit(solution)/shard_map/ppermute | solution.py:34
  170.2 2.5 %copy-start.25 = (f32[8,256]{1,0:T(8,128)}, f32[8,256]{1,0:T(8,128)S(1)}, u32[]{:S(2)}) copy-start(f32[8,256]{1,0:T(8,128)S(1)} %collective-permute-done.25.s2) | copy-start | bytes 24580
  170.2 2.5 %collective-permute-start.26 = (f32[8,256]{1,0:T(8,128)S(1)}, f32[8,256]{1,0:T(8,128)S(1)}, u32[]{:S(2)}, u32[]{:S(2)}) collective-permute-start(f32[8,256]{1,0:T(8,128)S(1)} %collective-permute-done.25.s2), channel_id=1, source_target_pairs={{0,1},{1,0},{2,3},{3,2},{4,5},{5,4},{6,7},{7,6},{8,9},{9,8},{10,11... | collective-permute-start | bytes 24584 | tf_op jit(solution)/shard_map/ppermute | solution.py:34
  171.8 0.8 copy-start.26
  172.6 0.6 copy-start.27
